TPU v7x, 32 devices: a whole 2x2x4 slice. The times are simulated.
32 devices in a mesh: lev: 2 (over x), lat: 16 (over z, y, core).
Axes of the slice: x: 2, y: 2, z: 4, core: 2. Of those that a mesh axis runs over, the one named last changes fastest.
Arguments:
- tokens: bfloat16 [8, 96, 24, 512], P('lev', 'lat'), may hold values from -6 to 6
- level_ids: int32 [8], P('lev'), may hold values from 0 to 12
- level_table: float32 [13, 512], replicated, may hold values from -6 to 6
- latent_query: bfloat16 [4, 512], replicated, may hold values from -360 to 360
- w_query: bfloat16 [512, 512], replicated, may hold values from -0.25 to 0.25
- w_kv: bfloat16 [512, 1024], replicated, may hold values from -0.25 to 0.25
- w_attn_out: bfloat16 [512, 512], replicated, may hold values from -0.25 to 0.25
- regions: int32 [96, 24, 4], P('lat', 'lev'), may hold values from 0 to 3
- gain_one: float32 [2, 512], replicated, may hold values from 0.25 to 1.75
- gain_two: float32 [2, 512], replicated, may hold values from 0.25 to 1.75
- w_qkv: bfloat16 [2, 512, 1536], P(None, 'lat'), may hold values from -0.25 to 0.25
- w_proj: bfloat16 [2, 512, 512], P(None, 'lat'), may hold values from -0.25 to 0.25
- w_up: bfloat16 [2, 512, 2048], P(None, 'lat'), may hold values from -0.25 to 0.25
- w_down: bfloat16 [2, 2048, 512], P(None, 'lat'), may hold values from -0.125 to 0.125
Outputs:
- grid_out: bfloat16 [96, 24, 4, 512], P('lat', 'lev')
Inputs may be any that keep to these rules, and one draw needn't show every extreme that they name: `regions`: within a window of the shifted grid, tokens attend only to tokens of the same region id.
All inputs are finite; a program needn't handle non-finite values.
Results may differ from a plain program's by a relative error of at most 0.018.
Values may be sent and summed in bfloat16 or wider, within the bound.
No kernel may reach another device: no remote copies, remote signals or barrier semaphores. Data moves between devices by JAX's collectives and lax.ppermute only.
A program may use at most 64 MiB of HBM per device.

v0:
```python
import functools

import jax
import jax.numpy as jnp
import numpy as np
from jax import lax
from jax.experimental import pallas as pl
from jax.experimental.pallas import tpu as pltpu
from jax.sharding import PartitionSpec as P


HEADS = 16
HD = 32
Q_LAT = 4
UNITS = 12
GROUP = 128 // HD

eps = 1e-05


BF = jnp.bfloat16
F32 = jnp.float32


def vspec():
    return pl.BlockSpec(memory_space=pltpu.VMEM)


def sspec():
    return pl.BlockSpec(memory_space=pltpu.SMEM)


def call(body, out_shape, args, smem=(), alias=None, scratch=(), limit=8):
    many = isinstance(out_shape, (tuple, list))
    return pl.pallas_call(
        body,
        out_shape=out_shape,
        in_specs=[sspec() if i in smem else vspec() for i in range(len(args))],
        out_specs=[vspec() for _ in out_shape] if many else vspec(),
        scratch_shapes=list(scratch),
        compiler_params=pltpu.CompilerParams(vmem_limit_bytes=limit << 20),
        input_output_aliases=alias or {},
    )(*args)


def dot(a, b, dims=((1,), (0,))):
    return lax.dot_general(a, b, (dims, ((), ())), preferred_element_type=F32)


def layer_norm(flat, gain):
    mean = jnp.mean(flat, -1, keepdims=True)
    centred = flat - mean
    var = jnp.mean(centred * centred, -1, keepdims=True)
    return centred * lax.rsqrt(var + eps) * gain


def pack_body(qkv, proj, up, down, *outs):
    width = proj.shape[-1]
    rows = proj.shape[1]
    for b, out in enumerate(outs):
        for u in range(3):
            out[u] = qkv[b, :, u * width : (u + 1) * width]
        out[3] = proj[b]
        for u in range(4):
            out[4 + u] = up[b, :, u * width : (u + 1) * width]
            out[8 + u] = down[b, u * rows : (u + 1) * rows, :]


def pack(w_qkv, w_proj, w_up, w_down):
    blocks, rows, width = w_proj.shape
    own = jax.ShapeDtypeStruct((UNITS, rows, width), BF)
    return call(pack_body, [own] * blocks, (w_qkv, w_proj, w_up, w_down))


def over(axis, fn, array):
    return lax.ppermute(array, axis, [(i, fn(i)) for i in range(lax.axis_size(axis))])


def place_body(*refs, count):
    where, table, refs = refs[0], refs[1], refs[2:]
    bufs, w = refs[:count], refs[-1]
    lat_size = w.shape[0] // UNITS
    for i, buf in enumerate(bufs):
        j = table[i, where[1]]
        for u in range(UNITS):
            w[u * lat_size + j if u < 8 else 8 * lat_size + 4 * j + (u - 8)] = buf[u]


def place(where, w, group):
    rows, width = group[0][0].shape[1:]
    whole = jax.ShapeDtypeStruct((UNITS * lax.axis_size("lat"), rows, width), BF)
    table = jnp.asarray(np.stack([at for _, at in group]), jnp.int32)
    args = [where, table] + [array for array, _ in group]
    body = functools.partial(place_body, count=len(group))
    if w is None:
        return call(body, whole, args, smem=(0, 1), limit=2)
    return call(body, whole, args + [w], smem=(0, 1), limit=2, alias={len(args): 0})


def gather(where, own, tie):
    size = lax.axis_size("lat")
    outer = size // 4
    order = [0] + list(range(1, outer, 2)) + list(range(2, outer, 2))[::-1]
    spot = {z: i for i, z in enumerate(order)}
    following = [order[(spot[z] + 1) % outer] for z in range(outer)]
    before = np.array([order[spot[z] - 1] for z in range(outer)])
    at = np.arange(size)
    array, tied = own, own
    w = place(where, None, [(own, at)])
    waiting = [(over("lat", lambda i: i ^ 1, own), at ^ 1)]
    for step in range(outer):
        last = step == outer - 1
        if not last:
            ahead = over("lat", lambda i: following[i // 4] * 4 + i % 4, array)
        across = over("lat", lambda i: i ^ 2, tied)
        fresh = [(across, at ^ 2)]
        if step:
            fresh.append((over("lat", lambda i: i ^ 1, tied), at ^ 1))
        w = place(where, w, waiting + ([(tied, at)] if step else []))
        waiting = fresh + [(over("lat", lambda i: i ^ 1, across), at ^ 3)]
        if not last:
            array = ahead
            tied, w = lax.optimization_barrier((ahead, w))
            if step == outer - 2:
                tied, tie = lax.optimization_barrier((tied, tie))
            at = before[at // 4] * 4 + at % 4
    return place(where, w, waiting), tie


def prep_body(lev, ids, source, tokens, table, own, send):
    slots, rows, cols, width = tokens.shape
    count = rows * cols // 2
    lanes = lax.broadcasted_iota(jnp.int32, (count, rows * cols), 1)
    here = source[...] + lev[0] * (cols // 2)
    there = source[...] + (1 - lev[0]) * (cols // 2)
    pick_own = (lanes == here).astype(BF)
    pick_send = (lanes == there).astype(BF)
    for s in range(slots):
        level = table[pl.ds(ids[s], 1), :]
        summed = (tokens[s].reshape(rows * cols, width).astype(F32) + level).astype(BF)
        send[s] = dot(pick_send, summed).astype(BF)
        own[s] = dot(pick_own, summed).astype(BF)


def encode_body(own, recv, latent_query, w_query, w_kv, w_out, out, kv, weights):
    slots_half, count, width = own.shape
    slots = 2 * slots_half
    half_rows = slots_half * count
    kv[:half_rows, :] = dot(own[...].reshape(half_rows, width), w_kv[...]).astype(BF)
    kv[half_rows:, :] = dot(recv[...].reshape(half_rows, width), w_kv[...]).astype(BF)
    queries = dot(latent_query[...], w_query[...]).astype(BF).astype(F32)
    qh = Q_LAT * HEADS
    head_row = lax.broadcasted_iota(jnp.int32, (HEADS, width), 0)
    head_lane = lax.broadcasted_iota(jnp.int32, (HEADS, width), 1) // HD
    select = (head_row == head_lane).astype(F32)
    block = jnp.concatenate([queries[q : q + 1] * select for q in range(Q_LAT)], 0).astype(BF)
    score = dot(kv[:, :width], block, ((1,), (1,))) * HD ** (-0.5)
    score = score.reshape(slots, count, qh)
    top = jnp.max(score, 0)
    weight = jnp.exp(score - top[None])
    weight = (weight / jnp.sum(weight, 0)[None]).reshape(slots * count, qh)
    high = weight.astype(BF)
    low = (weight - high.astype(F32)).astype(BF)
    weights[...] = jnp.concatenate([high, low], 1)
    row = lax.broadcasted_iota(jnp.int32, (2 * qh, width), 0)
    lane = lax.broadcasted_iota(jnp.int32, (2 * qh, width), 1) // HD
    for q in range(Q_LAT):
        spread = ((row == lane + q * HEADS) | (row == lane + q * HEADS + qh)).astype(BF)
        total = None
        for s in range(slots):
            at = slice(s * count, (s + 1) * count)
            part = dot(weights[at, :], spread) * kv[at, width:].astype(F32)
            total = part if total is None else total + part
        attended = total.astype(BF)
        out[q * count : (q + 1) * count, :] = (dot(attended, w_out[...]) + queries[q : q + 1]).astype(BF)


def block_body(*refs, masked, tokens_in, out_count):
    w, gain_a, gain_b, refs = refs[0], refs[1], refs[2], refs[3:]
    if masked:
        labels, refs = refs[0], refs[1:]
    ins, refs = refs[:tokens_in], refs[tokens_in:]
    outs, refs = refs[:out_count], refs[out_count:]
    x, ctx = refs
    width = x.shape[1]
    lat_size = w.shape[0] // UNITS

    def weight(unit, count=1):
        return w[unit * lat_size : (unit + count) * lat_size].reshape(count * width, width)

    if masked:
        piece = ins[0].shape[0] // 4
        for q in range(4):
            value = ins[q][...].astype(F32)
            x[q * 2 * piece : (q + 1) * 2 * piece, :] = value[piece : 3 * piece]
            base = 8 * piece + q * 2 * piece
            x[base : base + piece, :] = value[3 * piece :]
            x[base + piece : base + 2 * piece, :] = value[:piece]
    else:
        x[...] = ins[0][...].astype(F32)
    total = x.shape[0]
    tokens = total // 2
    normed = layer_norm(x[...], gain_a[...]).astype(BF)
    query = dot(normed, weight(0)).astype(BF)
    keys = dot(normed, weight(1)).astype(BF)
    vals = dot(normed, weight(2)).astype(BF)
    lane = lax.broadcasted_iota(jnp.int32, (tokens, 128), 1) // HD
    zero = jnp.zeros((tokens, 128), BF)
    for n in range(2):
        if masked:
            row = labels[n : n + 1, :].astype(F32)
            same = jnp.broadcast_to(row, (8, tokens)).T[:, :1] == row
        for g in range(width // 128):
            at = (slice(n * tokens, (n + 1) * tokens), slice(g * 128, (g + 1) * 128))
            q_g, k_g, v_g = query[at], keys[at], vals[at]
            weights, spread = [], []
            for h in range(GROUP):
                inside = lane == h
                k_h = jnp.where(inside, k_g, zero)
                score = dot(k_h, q_g, ((1,), (1,))) * HD ** (-0.5)
                if masked:
                    score = jnp.where(same, score, -1000000000.0)
                top = jnp.max(score, 0, keepdims=True)
                part = jnp.exp(score - top)
                part = part * (1.0 / jnp.sum(part, 0, keepdims=True))
                weights.append(part.astype(BF))
                spread.append(jnp.where(inside, v_g, zero))
            weights = jnp.concatenate(weights, 0)
            spread = jnp.concatenate(spread, 0)
            context = dot(spread, weights, ((0,), (0,)))
            ctx[at] = context.T.astype(BF)
    mixed = (x[...] + dot(ctx[...], weight(3))).astype(BF).astype(F32)
    normed_b = layer_norm(mixed, gain_b[...]).astype(BF)
    result = mixed
    down_all = weight(8, 4)
    for u in range(4):
        hidden = jax.nn.gelu(dot(normed_b, weight(4 + u))).astype(BF)
        result = result + dot(hidden, down_all[u * width : (u + 1) * width])
    result = result.astype(BF)
    x[...] = result.astype(F32)
    piece = total // 16
    if masked:
        for q in range(4):
            base = 8 * piece + q * 2 * piece
            parts = [
                x[base + piece : base + 2 * piece, :],
                x[q * 2 * piece : (q + 1) * 2 * piece, :],
                x[base : base + piece, :],
            ]
            outs[q][...] = jnp.concatenate(parts, 0).astype(BF)
    else:
        for q in range(4):
            parts = [x[(4 * k + q) * piece : (4 * k + q + 1) * piece, :] for k in range(Q_LAT)]
            outs[q][...] = jnp.concatenate(parts, 0).astype(BF)


def swin_block(w, gain_a, gain_b, tokens, labels):
    width = w.shape[-1]
    total = sum(t.shape[0] for t in tokens)
    args = [w, gain_a, gain_b] + list(labels) + list(tokens)
    body = functools.partial(block_body, masked=len(labels) > 0, tokens_in=len(tokens), out_count=4)
    quad = jax.ShapeDtypeStruct((total // 4, width), BF)
    scratch = [pltpu.VMEM((total, width), F32), pltpu.VMEM((total, width), BF)]
    return call(body, [quad] * 4, args, scratch=scratch, limit=10)


def roll_quarters(quarters, sign):
    size, sides = lax.axis_size("lat"), lax.axis_size("lev")
    pairs = [(i, (i + sign) % size) for i in range(size)]
    flat = [
        (a * size + i, ((a + sign) % sides) * size + (i + sign) % size) for a in range(sides) for i in range(size)
    ]
    one = lax.ppermute(quarters[1 if sign < 0 else 2], "lat", pairs)
    two = over("lev", lambda i: (i + sign) % sides, quarters[2 if sign < 0 else 1])
    three = lax.ppermute(quarters[0 if sign < 0 else 3], ("lev", "lat"), flat)
    if sign < 0:
        return quarters[3], two, one, three
    return three, one, two, quarters[0]


def unquarter_body(pick, *refs):
    quarters, out = refs[:4], refs[4]
    rows, cols, levels, _ = out.shape
    stacked = jnp.concatenate([q[...] for q in quarters], 0)
    total = stacked.shape[0]
    lanes = lax.broadcasted_iota(jnp.int32, (total, total), 1)
    onehot = (lanes == pick[...]).astype(BF)
    flat = dot(onehot, stacked)
    for r in range(rows):
        for c in range(cols):
            at = (r * cols + c) * levels
            out[r, c] = flat[at : at + levels].astype(BF)


def quarter_order(rows, cols):
    grid = np.arange(rows * cols).reshape(2, rows // 2, 2, cols // 2)
    return grid.transpose(0, 2, 1, 3).reshape(-1)


def local(
    tokens,
    level_ids,
    level_table,
    latent_query,
    w_query,
    w_kv,
    w_attn_out,
    regions,
    gain_one,
    gain_two,
    w_qkv,
    w_proj,
    w_up,
    w_down,
):
    slots, rows, cols_all, width = tokens.shape
    cols = cols_all // lax.axis_size("lev")
    count = rows * cols
    lev = lax.axis_index("lev").astype(jnp.int32).reshape(1)
    where = jnp.stack([lax.axis_index("lev"), lax.axis_index("lat")]).astype(jnp.int32)
    packed = pack(w_qkv, w_proj, w_up, w_down)
    order = quarter_order(rows, cols)
    source = jnp.asarray((order // cols * cols_all + order % cols).reshape(-1, 1), jnp.int32)
    part = jax.ShapeDtypeStruct((slots, count, width), BF)
    own, send = call(prep_body, [part, part], (lev, level_ids, source, tokens, level_table), smem=(0, 1))
    recv = over("lev", lambda i: i ^ 1, send)
    state = call(
        encode_body,
        jax.ShapeDtypeStruct((Q_LAT * count, width), BF),
        (own, recv, latent_query, w_query, w_kv, w_attn_out),
        scratch=[pltpu.VMEM((2 * slots * count, 2 * width), BF), pltpu.VMEM((2 * slots * count, 128), BF)],
        limit=16,
    )
    labels = regions.reshape(2, rows // 2, 2, cols // 2, 2, 2).transpose(4, 0, 2, 5, 1, 3).reshape(2, -1)
    first, (state, labels) = gather(where, packed[0], (state, labels))
    plain = swin_block(first, gain_one[:1], gain_two[:1], [state], ())
    second, plain = gather(where, packed[1], tuple(plain))
    rolled = roll_quarters(plain, -1)
    shifted = swin_block(second, gain_one[1:], gain_two[1:], rolled, (labels,))
    quarters = roll_quarters(shifted, 1)
    inverse = np.argsort(order)
    per = count // 4
    where = inverse[:, None] // per * (Q_LAT * per) + np.arange(Q_LAT)[None] * per + inverse[:, None] % per
    pick = jnp.asarray(where.reshape(-1, 1), jnp.int32)
    return call(unquarter_body, jax.ShapeDtypeStruct((rows, cols, Q_LAT, width), BF), (pick,) + tuple(quarters))


def solution(mesh):
    in_specs = (
        P("lev", "lat", None, None),
        P("lev"),
        P(),
        P(),
        P(),
        P(),
        P(),
        P("lat", "lev", None),
        P(),
        P(),
        P(None, "lat", None),
        P(None, "lat", None),
        P(None, "lat", None),
        P(None, "lat", None),
    )
    out_specs = P("lat", "lev", None, None)

    return jax.shard_map(local, mesh=mesh, in_specs=in_specs, out_specs=out_specs, check_vma=False)
```

profile of v0, /device:TPU:0, one launch (start us, length us, event | category | flops | bytes accessed | tf_op | source)
XLA Modules:
  0.0 128.2 jit_solution(15497342918541562091)
XLA Ops:
  0.0 1.0 copy-done.20
  1.0 0.9 copy-done.21
  1.9 0.9 copy-done.22
  2.8 0.8 copy-done.24
  3.7 0.8 shard_map.262
  5.0 2.6 %collective-permute-start.9 = (bf16[12,32,512]{2,1,0:T(8,128)(2,1)S(1)}, bf16[12,32,512]{2,1,0:T(8,128)(2,1)S(1)}, u32[]{:S(2)}, u32[]{:S(2)}) collective-permute-start(bf16[12,32,512]{2,1,0:T(8,128)(2,1)S(1)} %get-tuple-element.43.refs_2_), channel_id=1, source_target_pairs={{0,4},{1,5},{2,6},{3,7},{4,12},{5,13},{6,14},{7,15},{8,0},{9,1},{1... | collective-permute-start | bytes 1179656 | tf_op jit(solution)/shard_map/ppermute | solution.py:76
  7.5 1.5 %collective-permute-start.16 = (bf16[12,32,512]{2,1,0:T(8,128)(2,1)S(1)}, bf16[12,32,512]{2,1,0:T(8,128)(2,1)}, u32[]{:S(2)}, u32[]{:S(2)}) collective-permute-start(bf16[12,32,512]{2,1,0:T(8,128)(2,1)S(1)} %get-tuple-element.43.refs_2_), channel_id=1, source_target_pairs={{0,2},{1,3},{2,0},{3,1},{4,6},{5,7},{6,4},{7,5},{8,10},{9,11},{10,... | collective-permute-start | bytes 1179656 | tf_op jit(solution)/shard_map/ppermute | solution.py:76
  9.1 1.1 copy-done.5
  10.1 0.8 copy-done.25
  10.9 0.8 copy-done.26
  11.7 0.7 copy-done.34
  12.3 0.9 shard_map.271
  13.3 0.7 copy-done.16
  14.0 1.5 %collective-permute-start.18 = (bf16[4,72,512]{2,1,0:T(8,128)(2,1)S(1)}, bf16[4,72,512]{2,1,0:T(8,128)(2,1)S(1)}, u32[]{:S(2)}, u32[]{:S(2)}) collective-permute-start(bf16[4,72,512]{2,1,0:T(8,128)(2,1)S(1)} %get-tuple-element.50), channel_id=1, source_target_pairs={{0,16},{16,0},{1,17},{17,1},{2,18},{18,2},{3,19},{19,3},{4,20},{20... | collective-permute-start | bytes 884744 | tf_op jit(solution)/shard_map/ppermute | solution.py:76
  15.5 2.6 %collective-permute-start = (bf16[12,32,512]{2,1,0:T(8,128)(2,1)}, bf16[12,32,512]{2,1,0:T(8,128)(2,1)S(1)}, u32[]{:S(2)}, u32[]{:S(2)}) collective-permute-start(bf16[12,32,512]{2,1,0:T(8,128)(2,1)} %get-tuple-element.37.refs_2_), channel_id=1, source_target_pairs={{0,4},{1,5},{2,6},{3,7},{4,12},{5,13},{6,14},{7,15},{8,0},{9,1},{1... | collective-permute-start | bytes 1179656 | tf_op jit(solution)/shard_map/ppermute | solution.py:76
  18.1 0.7 copy-done.33
  18.8 0.6 shard_map.267.refs_3_
  19.4 0.6 shard_map.268.refs_5_
  20.0 2.7 %copy-done.1 = bf16[192,32,512]{2,1,0:T(8,128)(2,1)} copy-done((bf16[192,32,512]{2,1,0:T(8,128)(2,1)}, bf16[192,32,512]{2,1,0:T(8,128)(2,1)S(1)}, u32[]{:S(2)}) %copy-start.1) | copy-done | bytes 6291480
  23.4 0.7 copy-done.18
  24.1 1.3 %collective-permute-start.7 = (bf16[12,32,512]{2,1,0:T(8,128)(2,1)}, bf16[12,32,512]{2,1,0:T(8,128)(2,1)}, u32[]{:S(2)}, u32[]{:S(2)}) collective-permute-start(bf16[12,32,512]{2,1,0:T(8,128)(2,1)} %get-tuple-element.37.refs_2_), channel_id=1, source_target_pairs={{0,2},{1,3},{2,0},{3,1},{4,6},{5,7},{6,4},{7,5},{8,10},{9,11},{10,... | collective-permute-start | bytes 1179656 | tf_op jit(solution)/shard_map/ppermute | solution.py:76
  25.4 1.8 %collective-permute-start.10 = (bf16[12,32,512]{2,1,0:T(8,128)(2,1)S(1)}, bf16[12,32,512]{2,1,0:T(8,128)(2,1)S(1)}, u32[]{:S(2)}, u32[]{:S(2)}) collective-permute-start(bf16[12,32,512]{2,1,0:T(8,128)(2,1)S(1)} %collective-permute-done.9.refs_4_), channel_id=1, source_target_pairs={{0,4},{1,5},{2,6},{3,7},{4,12},{5,13},{6,14},{7,15},{8,0},{9,1},{1... | collective-permute-start | bytes 1179656 | tf_op jit(solution)/shard_map/ppermute | solution.py:76
  27.2 0.8 copy-done.10
  28.5 1.0 shard_map.263.refs_3_
  29.6 5.2 %collective-permute-done.13.refs_2_ = bf16[12,32,512]{2,1,0:T(8,128)(2,1)} collective-permute-done((bf16[12,32,512]{2,1,0:T(8,128)(2,1)S(1)}, bf16[12,32,512]{2,1,0:T(8,128)(2,1)}, u32[]{:S(2)}, u32[]{:S(2)}) %collective-permute-start.13) | collective-permute-done | bytes 393248 | tf_op jit(solution)/shard_map/ppermute | solution.py:76
  34.8 0.6 shard_map.264.refs_5_
  35.4 2.6 %copy-done = bf16[192,32,512]{2,1,0:T(8,128)(2,1)} copy-done((bf16[192,32,512]{2,1,0:T(8,128)(2,1)}, bf16[192,32,512]{2,1,0:T(8,128)(2,1)S(1)}, u32[]{:S(2)}) %copy-start) | copy-done | bytes 6291480
  38.0 4.2 %collective-permute-done.7.refs_2_ = bf16[12,32,512]{2,1,0:T(8,128)(2,1)} collective-permute-done((bf16[12,32,512]{2,1,0:T(8,128)(2,1)}, bf16[12,32,512]{2,1,0:T(8,128)(2,1)}, u32[]{:S(2)}, u32[]{:S(2)}) %collective-permute-start.7) | collective-permute-done | bytes 393248 | tf_op jit(solution)/shard_map/ppermute | solution.py:76
  42.2 0.5 collective-permute-start.4
  43.2 0.7 copy-done.14
  43.9 0.7 copy-done.12
  45.3 1.0 copy-done.17
  46.2 1.0 copy-done.19
  47.2 3.1 %shard_map.272.refs_3_ = bf16[288,512]{1,0:T(8,128)(2,1)S(1)} custom-call(bf16[4,72,512]{2,1,0:T(8,128)(2,1)S(1)} %copy-done.17, bf16[4,72,512]{2,1,0:T(8,128)(2,1)S(1)} %copy-done.19, bf16[4,512]{1,0:T(4,128)(2,1)S(1)} %copy-done.31, bf16[512,512]{1,0:T(8,128)(2,1)S(1)} %copy-done.6, bf16[512,1024]{1,0:T(8,128)(2,1)S(1)} %copy-done.4, ...), custom_call_target="tpu_custom_call" | custom-call | tf_op jit(solution)/shard_map/pallas_call | solution.py:35
  50.3 2.8 %copy-done.2 = bf16[192,32,512]{2,1,0:T(8,128)(2,1)S(1)} copy-done((bf16[192,32,512]{2,1,0:T(8,128)(2,1)S(1)}, bf16[192,32,512]{2,1,0:T(8,128)(2,1)}, u32[]{:S(2)}) %copy-start.2) | copy-done | bytes 6291480
  53.1 1.0 copy-done.9
  54.1 1.0 copy-done.15
  55.1 1.2 shard_map.269.refs_6_
  56.7 1.6 %shard_map.270.refs_6_ = bf16[192,32,512]{2,1,0:T(8,128)(2,1)S(1)} custom-call(s32[2]{0:T(128)S(1)} %pad_add_fusion.refs_0_, s32[4,16]{1,0:T(4,128)S(1)} %copy-done.29, bf16[12,32,512]{2,1,0:T(8,128)(2,1)} %collective-permute-done.13.refs_2_, bf16[12,32,512]{2,1,0:T(8,128)(2,1)S(1)} %copy-done.13, ...), custom_call_target="tpu_custom_call", output_to_operand_aliasing={{}: (6, {})} | custom-call | tf_op jit(solution)/shard_map/pallas_call | solution.py:35
  58.3 2.7 %copy-done.3 = bf16[192,32,512]{2,1,0:T(8,128)(2,1)} copy-done((bf16[192,32,512]{2,1,0:T(8,128)(2,1)}, bf16[192,32,512]{2,1,0:T(8,128)(2,1)S(1)}, u32[]{:S(2)}) %copy-start.3) | copy-done | bytes 6291480
  61.0 1.5 %collective-permute-start.22 = (bf16[12,32,512]{2,1,0:T(8,128)(2,1)S(1)}, bf16[12,32,512]{2,1,0:T(8,128)(2,1)S(1)}, u32[]{:S(2)}, u32[]{:S(2)}) collective-permute-start(bf16[12,32,512]{2,1,0:T(8,128)(2,1)S(1)} %collective-permute-done.10.refs_5_), channel_id=1, source_target_pairs={{0,2},{1,3},{2,0},{3,1},{4,6},{5,7},{6,4},{7,5},{8,10},{9,11},{10,... | collective-permute-start | bytes 1179656 | tf_op jit(solution)/shard_map/ppermute | solution.py:76
  62.6 0.5 collective-permute-start.19
  63.2 1.6 %collective-permute-start.2 = (bf16[12,32,512]{2,1,0:T(8,128)(2,1)S(1)}, bf16[12,32,512]{2,1,0:T(8,128)(2,1)S(1)}, u32[]{:S(2)}, u32[]{:S(2)}) collective-permute-start(bf16[12,32,512]{2,1,0:T(8,128)(2,1)S(1)} %collective-permute-done.1.refs_5_), channel_id=1, source_target_pairs={{0,4},{1,5},{2,6},{3,7},{4,12},{5,13},{6,14},{7,15},{8,0},{9,1},{1... | collective-permute-start | bytes 1179656 | tf_op jit(solution)/shard_map/ppermute | solution.py:76
  64.7 8.3 %collective-permute-done.22.refs_2_ = bf16[12,32,512]{2,1,0:T(8,128)(2,1)S(1)} collective-permute-done((bf16[12,32,512]{2,1,0:T(8,128)(2,1)S(1)}, bf16[12,32,512]{2,1,0:T(8,128)(2,1)S(1)}, u32[]{:S(2)}, u32[]{:S(2)}) %collective-permute-start.22) | collective-permute-done | bytes 393248 | tf_op jit(solution)/shard_map/ppermute | solution.py:76
  73.5 7.3 %collective-permute-done.19.refs_2_ = bf16[12,32,512]{2,1,0:T(8,128)(2,1)S(1)} collective-permute-done((bf16[12,32,512]{2,1,0:T(8,128)(2,1)}, bf16[12,32,512]{2,1,0:T(8,128)(2,1)S(1)}, u32[]{:S(2)}, u32[]{:S(2)}) %collective-permute-start.19) | collective-permute-done | bytes 393248 | tf_op jit(solution)/shard_map/ppermute | solution.py:76
  80.8 1.4 %shard_map.265.refs_6_ = bf16[192,32,512]{2,1,0:T(8,128)(2,1)S(1)} custom-call(s32[2]{0:T(128)S(1)} %pad_add_fusion.refs_0_, s32[3,16]{1,0:T(4,128)S(1)} %copy-done.30, bf16[12,32,512]{2,1,0:T(8,128)(2,1)} %collective-permute-done.7.refs_2_, bf16[12,32,512]{2,1,0:T(8,128)(2,1)} %collective-permute-done.8.refs_3_, ...), custom_call_target="tpu_custom_call", output_to_operand_aliasing={{}: (5, {})} | custom-call | tf_op jit(solution)/shard_map/pallas_call | solution.py:35
  82.2 1.6 %collective-permute-start.28 = (bf16[12,32,512]{2,1,0:T(8,128)(2,1)S(1)}, bf16[12,32,512]{2,1,0:T(8,128)(2,1)S(1)}, u32[]{:S(2)}, u32[]{:S(2)}) collective-permute-start(bf16[12,32,512]{2,1,0:T(8,128)(2,1)S(1)} %collective-permute-done.1.refs_5_), channel_id=1, source_target_pairs={{0,2},{1,3},{2,0},{3,1},{4,6},{5,7},{6,4},{7,5},{8,10},{9,11},{10,... | collective-permute-start | bytes 1179656 | tf_op jit(solution)/shard_map/ppermute | solution.py:76
  83.8 1.3 shard_map.266.refs_6_
  85.5 1.1 shard_map.273.refs_5_
  86.7 0.7 shard_map.274.refs_0_
  87.3 6.1 %shard_map.275 = (bf16[72,512]{1,0:T(8,128)(2,1)S(1)}, bf16[72,512]{1,0:T(8,128)(2,1)S(1)}, bf16[72,512]{1,0:T(8,128)(2,1)S(1)}, bf16[72,512]{1,0:T(8,128)(2,1)S(1)}) custom-call(bf16[192,32,512]{2,1,0:T(8,128)(2,1)S(1)} %shard_map.274.refs_0_, f32[1,512]{1,0:T(1,128)S(1)} %get-tuple-element.73.refs_1_, f32[1,512]{1,0:T(1,128)S(1)} %get-tuple-element.70.refs_2_, ...), custom_call_target="tpu_custom_call" | custom-call | tf_op jit(solution)/shard_map/pallas_call | solution.py:35
  93.5 0.7 collective-permute-start.25
  94.7 10.1 %collective-permute-done.25.refs_2_ = bf16[12,32,512]{2,1,0:T(8,128)(2,1)S(1)} collective-permute-done((bf16[12,32,512]{2,1,0:T(8,128)(2,1)S(1)}, bf16[12,32,512]{2,1,0:T(8,128)(2,1)S(1)}, u32[]{:S(2)}, u32[]{:S(2)}) %collective-permute-start.25) | collective-permute-done | bytes 393248 | tf_op jit(solution)/shard_map/ppermute | solution.py:76
  104.8 0.7 collective-permute-start.31
  105.4 3.4 %collective-permute-start.32 = (bf16[72,512]{1,0:T(8,128)(2,1)S(1)}, bf16[72,512]{1,0:T(8,128)(2,1)S(1)}, u32[]{:S(2)}, u32[]{:S(2)}) collective-permute-start(bf16[72,512]{1,0:T(8,128)(2,1)S(1)} %get-tuple-element.63), channel_id=1, source_target_pairs={{0,15},{1,0},{2,1},{3,2},{4,3},{5,4},{6,5},{7,6},{8,7},{9,8},{10,9... | collective-permute-start | bytes 221192 | tf_op jit(solution)/shard_map/ppermute | solution.py:273
  108.9 1.2 collective-permute-start.33
  110.1 0.7 shard_map.276.refs_5_
  110.8 0.7 shard_map.277.refs_0_
  111.5 1.2 collective-permute-done.33.refs_7_
  112.6 6.2 %shard_map.278 = (bf16[72,512]{1,0:T(8,128)(2,1)S(1)}, bf16[72,512]{1,0:T(8,128)(2,1)S(1)}, bf16[72,512]{1,0:T(8,128)(2,1)S(1)}, bf16[72,512]{1,0:T(8,128)(2,1)S(1)}) custom-call(bf16[192,32,512]{2,1,0:T(8,128)(2,1)S(1)} %shard_map.277.refs_0_, f32[1,512]{1,0:T(1,128)S(1)} %get-tuple-element.74.refs_1_, f32[1,512]{1,0:T(1,128)S(1)} %get-tuple-element.69.refs_2_, ...), custom_call_target="tpu_custom_call" | custom-call | tf_op jit(solution)/shard_map/pallas_call | solution.py:35
  119.0 1.6 %collective-permute-start.36 = (bf16[72,512]{1,0:T(8,128)(2,1)S(1)}, bf16[72,512]{1,0:T(8,128)(2,1)S(1)}, u32[]{:S(2)}, u32[]{:S(2)}) collective-permute-start(bf16[72,512]{1,0:T(8,128)(2,1)S(1)} %get-tuple-element.67), channel_id=1, source_target_pairs={{0,16},{16,0},{1,17},{17,1},{2,18},{18,2},{3,19},{19,3},{4,20},{20... | collective-permute-start | bytes 221192 | tf_op jit(solution)/shard_map/ppermute | solution.py:76
  120.6 5.7 %collective-permute-done.34.refs_0_ = bf16[72,512]{1,0:T(8,128)(2,1)S(1)} collective-permute-done((bf16[72,512]{1,0:T(8,128)(2,1)S(1)}, bf16[72,512]{1,0:T(8,128)(2,1)S(1)}, u32[]{:S(2)}, u32[]{:S(2)}) %collective-permute-start.34) | collective-permute-done | bytes 73760 | tf_op jit(solution)/shard_map/ppermute | solution.py:275
  126.3 0.8 collective-permute-done.35.refs_1_
  127.1 1.1 shard_map.279
  (119 shorter events, 4.8 us)
Async XLA Ops:
  0.0 19.4 %copy-start.32 = (s32[1,16]{1,0:T(1,128)S(1)}, s32[1,16]{1,0:T(1,128)}, u32[]{:S(2)}) copy-start(s32[1,16]{1,0:T(1,128)} %constant.27.clone.refs_1_) | copy-start | bytes 196
  4.5 11.0 %collective-permute-start.12 = (bf16[12,32,512]{2,1,0:T(8,128)(2,1)S(1)}, bf16[12,32,512]{2,1,0:T(8,128)(2,1)S(1)}, u32[]{:S(2)}, u32[]{:S(2)}) collective-permute-start(bf16[12,32,512]{2,1,0:T(8,128)(2,1)S(1)} %get-tuple-element.43.refs_2_), channel_id=1, source_target_pairs={{0,1},{1,0},{2,3},{3,2},{4,5},{5,4},{6,7},{7,6},{8,9},{9,8},{10,11... | collective-permute-start | bytes 1179656 | tf_op jit(solution)/shard_map/ppermute | solution.py:76
  5.0 17.7 %collective-permute-start.9 = (bf16[12,32,512]{2,1,0:T(8,128)(2,1)S(1)}, bf16[12,32,512]{2,1,0:T(8,128)(2,1)S(1)}, u32[]{:S(2)}, u32[]{:S(2)}) collective-permute-start(bf16[12,32,512]{2,1,0:T(8,128)(2,1)S(1)} %get-tuple-element.43.refs_2_), channel_id=1, source_target_pairs={{0,4},{1,5},{2,6},{3,7},{4,12},{5,13},{6,14},{7,15},{8,0},{9,1},{1... | collective-permute-start | bytes 1179656 | tf_op jit(solution)/shard_map/ppermute | solution.py:76
  7.5 17.9 %collective-permute-start.16 = (bf16[12,32,512]{2,1,0:T(8,128)(2,1)S(1)}, bf16[12,32,512]{2,1,0:T(8,128)(2,1)}, u32[]{:S(2)}, u32[]{:S(2)}) collective-permute-start(bf16[12,32,512]{2,1,0:T(8,128)(2,1)S(1)} %get-tuple-element.43.refs_2_), channel_id=1, source_target_pairs={{0,2},{1,3},{2,0},{3,1},{4,6},{5,7},{6,4},{7,5},{8,10},{9,11},{10,... | collective-permute-start | bytes 1179656 | tf_op jit(solution)/shard_map/ppermute | solution.py:76
  9.1 18.1 %collective-permute-start.3 = (bf16[12,32,512]{2,1,0:T(8,128)(2,1)}, bf16[12,32,512]{2,1,0:T(8,128)(2,1)S(1)}, u32[]{:S(2)}, u32[]{:S(2)}) collective-permute-start(bf16[12,32,512]{2,1,0:T(8,128)(2,1)} %get-tuple-element.37.refs_2_), channel_id=1, source_target_pairs={{0,1},{1,0},{2,3},{3,2},{4,5},{5,4},{6,7},{7,6},{8,9},{9,8},{10,11... | collective-permute-start | bytes 1179656 | tf_op jit(solution)/shard_map/ppermute | solution.py:76
  9.1 1.1 copy-start.5
  14.0 9.4 %collective-permute-start.18 = (bf16[4,72,512]{2,1,0:T(8,128)(2,1)S(1)}, bf16[4,72,512]{2,1,0:T(8,128)(2,1)S(1)}, u32[]{:S(2)}, u32[]{:S(2)}) collective-permute-start(bf16[4,72,512]{2,1,0:T(8,128)(2,1)S(1)} %get-tuple-element.50), channel_id=1, source_target_pairs={{0,16},{16,0},{1,17},{17,1},{2,18},{18,2},{3,19},{19,3},{4,20},{20... | collective-permute-start | bytes 884744 | tf_op jit(solution)/shard_map/ppermute | solution.py:76
  15.5 12.5 %collective-permute-start = (bf16[12,32,512]{2,1,0:T(8,128)(2,1)}, bf16[12,32,512]{2,1,0:T(8,128)(2,1)S(1)}, u32[]{:S(2)}, u32[]{:S(2)}) collective-permute-start(bf16[12,32,512]{2,1,0:T(8,128)(2,1)} %get-tuple-element.37.refs_2_), channel_id=1, source_target_pairs={{0,4},{1,5},{2,6},{3,7},{4,12},{5,13},{6,14},{7,15},{8,0},{9,1},{1... | collective-permute-start | bytes 1179656 | tf_op jit(solution)/shard_map/ppermute | solution.py:76
  20.0 2.7 %copy-start.1 = (bf16[192,32,512]{2,1,0:T(8,128)(2,1)}, bf16[192,32,512]{2,1,0:T(8,128)(2,1)S(1)}, u32[]{:S(2)}) copy-start(bf16[192,32,512]{2,1,0:T(8,128)(2,1)S(1)} %shard_map.268.refs_5_) | copy-start | bytes 18874372
  22.7 12.7 %copy-start.8 = (bf16[12,32,512]{2,1,0:T(8,128)(2,1)}, bf16[12,32,512]{2,1,0:T(8,128)(2,1)S(1)}, u32[]{:S(2)}) copy-start(bf16[12,32,512]{2,1,0:T(8,128)(2,1)S(1)} %collective-permute-done.9.refs_4_) | copy-start | bytes 1179652
  22.7 12.1 %collective-permute-start.13 = (bf16[12,32,512]{2,1,0:T(8,128)(2,1)S(1)}, bf16[12,32,512]{2,1,0:T(8,128)(2,1)}, u32[]{:S(2)}, u32[]{:S(2)}) collective-permute-start(bf16[12,32,512]{2,1,0:T(8,128)(2,1)S(1)} %collective-permute-done.9.refs_4_), channel_id=1, source_target_pairs={{0,2},{1,3},{2,0},{3,1},{4,6},{5,7},{6,4},{7,5},{8,10},{9,11},{10,... | collective-permute-start | bytes 1179656 | tf_op jit(solution)/shard_map/ppermute | solution.py:76
  24.1 18.1 %collective-permute-start.7 = (bf16[12,32,512]{2,1,0:T(8,128)(2,1)}, bf16[12,32,512]{2,1,0:T(8,128)(2,1)}, u32[]{:S(2)}, u32[]{:S(2)}) collective-permute-start(bf16[12,32,512]{2,1,0:T(8,128)(2,1)} %get-tuple-element.37.refs_2_), channel_id=1, source_target_pairs={{0,2},{1,3},{2,0},{3,1},{4,6},{5,7},{6,4},{7,5},{8,10},{9,11},{10,... | collective-permute-start | bytes 1179656 | tf_op jit(solution)/shard_map/ppermute | solution.py:76
  25.4 17.3 %collective-permute-start.10 = (bf16[12,32,512]{2,1,0:T(8,128)(2,1)S(1)}, bf16[12,32,512]{2,1,0:T(8,128)(2,1)S(1)}, u32[]{:S(2)}, u32[]{:S(2)}) collective-permute-start(bf16[12,32,512]{2,1,0:T(8,128)(2,1)S(1)} %collective-permute-done.9.refs_4_), channel_id=1, source_target_pairs={{0,4},{1,5},{2,6},{3,7},{4,12},{5,13},{6,14},{7,15},{8,0},{9,1},{1... | collective-permute-start | bytes 1179656 | tf_op jit(solution)/shard_map/ppermute | solution.py:76
  28.0 15.2 %collective-permute-start.17 = (bf16[12,32,512]{2,1,0:T(8,128)(2,1)}, bf16[12,32,512]{2,1,0:T(8,128)(2,1)S(1)}, u32[]{:S(2)}, u32[]{:S(2)}) collective-permute-start(bf16[12,32,512]{2,1,0:T(8,128)(2,1)} %collective-permute-done.16.refs_2_), channel_id=1, source_target_pairs={{0,1},{1,0},{2,3},{3,2},{4,5},{5,4},{6,7},{7,6},{8,9},{9,8},{10,11... | collective-permute-start | bytes 1179656 | tf_op jit(solution)/shard_map/ppermute | solution.py:76
  28.0 6.8 %copy-start.11 = (bf16[12,32,512]{2,1,0:T(8,128)(2,1)S(1)}, bf16[12,32,512]{2,1,0:T(8,128)(2,1)}, u32[]{:S(2)}) copy-start(bf16[12,32,512]{2,1,0:T(8,128)(2,1)} %copy-done.10) | copy-start | bytes 1179652
  28.0 15.9 %collective-permute-start.14 = (bf16[12,32,512]{2,1,0:T(8,128)(2,1)S(1)}, bf16[12,32,512]{2,1,0:T(8,128)(2,1)S(1)}, u32[]{:S(2)}, u32[]{:S(2)}) collective-permute-start(bf16[12,32,512]{2,1,0:T(8,128)(2,1)S(1)} %collective-permute-done.9.refs_4_), channel_id=1, source_target_pairs={{0,1},{1,0},{2,3},{3,2},{4,5},{5,4},{6,7},{7,6},{8,9},{9,8},{10,11... | collective-permute-start | bytes 1179656 | tf_op jit(solution)/shard_map/ppermute | solution.py:76
  29.5 15.4 %copy-start.35 = (s32[6,12,4]{1,2,0:T(4,128)S(1)}, s32[6,12,4]{1,2,0:T(4,128)}, u32[]{:S(2)}) copy-start(s32[6,12,4]{1,2,0:T(4,128)} %param.35) | copy-start | bytes 3460
  29.6 15.6 %copy-start.4 = (bf16[512,1024]{1,0:T(8,128)(2,1)S(1)}, bf16[512,1024]{1,0:T(8,128)(2,1)}, u32[]{:S(2)}) copy-start(bf16[512,1024]{1,0:T(8,128)(2,1)} %w_kv.1) | copy-start | bytes 3145732
  29.6 15.6 %copy-start.6 = (bf16[512,512]{1,0:T(8,128)(2,1)S(1)}, bf16[512,512]{1,0:T(8,128)(2,1)}, u32[]{:S(2)}) copy-start(bf16[512,512]{1,0:T(8,128)(2,1)} %w_query.1) | copy-start | bytes 1572868
  29.6 15.6 %copy-start.7 = (bf16[512,512]{1,0:T(8,128)(2,1)S(1)}, bf16[512,512]{1,0:T(8,128)(2,1)}, u32[]{:S(2)}) copy-start(bf16[512,512]{1,0:T(8,128)(2,1)} %w_out.1) | copy-start | bytes 1572868
  29.6 15.6 %copy-start.31 = (bf16[4,512]{1,0:T(4,128)(2,1)S(1)}, bf16[4,512]{1,0:T(4,128)(2,1)}, u32[]{:S(2)}) copy-start(bf16[4,512]{1,0:T(4,128)(2,1)} %latent_query.1) | copy-start | bytes 12292
  29.6 20.7 %copy-start.30 = (s32[3,16]{1,0:T(4,128)S(1)}, s32[3,16]{1,0:T(4,128)}, u32[]{:S(2)}) copy-start(s32[3,16]{1,0:T(4,128)} %constant.28.clone.refs_1_) | copy-start | bytes 580
  34.8 21.6 %collective-permute-start.15 = (bf16[12,32,512]{2,1,0:T(8,128)(2,1)}, bf16[12,32,512]{2,1,0:T(8,128)(2,1)}, u32[]{:S(2)}, u32[]{:S(2)}) collective-permute-start(bf16[12,32,512]{2,1,0:T(8,128)(2,1)} %collective-permute-done.13.refs_2_), channel_id=1, source_target_pairs={{0,1},{1,0},{2,3},{3,2},{4,5},{5,4},{6,7},{7,6},{8,9},{9,8},{10,11... | collective-permute-start | bytes 1179656 | tf_op jit(solution)/shard_map/ppermute | solution.py:76
  35.4 2.6 %copy-start = (bf16[192,32,512]{2,1,0:T(8,128)(2,1)}, bf16[192,32,512]{2,1,0:T(8,128)(2,1)S(1)}, u32[]{:S(2)}) copy-start(bf16[192,32,512]{2,1,0:T(8,128)(2,1)S(1)} %shard_map.264.refs_5_) | copy-start | bytes 18874372
  42.2 18.9 %collective-permute-start.4 = (bf16[12,32,512]{2,1,0:T(8,128)(2,1)S(1)}, bf16[12,32,512]{2,1,0:T(8,128)(2,1)}, u32[]{:S(2)}, u32[]{:S(2)}) collective-permute-start(bf16[12,32,512]{2,1,0:T(8,128)(2,1)S(1)} %collective-permute-done.refs_4_), channel_id=1, source_target_pairs={{0,2},{1,3},{2,0},{3,1},{4,6},{5,7},{6,4},{7,5},{8,10},{9,11},{10,... | collective-permute-start | bytes 1179656 | tf_op jit(solution)/shard_map/ppermute | solution.py:76
  42.7 19.9 %collective-permute-start.11 = (bf16[12,32,512]{2,1,0:T(8,128)(2,1)S(1)}, bf16[12,32,512]{2,1,0:T(8,128)(2,1)}, u32[]{:S(2)}, u32[]{:S(2)}) collective-permute-start(bf16[12,32,512]{2,1,0:T(8,128)(2,1)S(1)} %collective-permute-done.10.refs_5_), channel_id=1, source_target_pairs={{0,4},{1,5},{2,6},{3,7},{4,12},{5,13},{6,14},{7,15},{8,0},{9,1},{1... | collective-permute-start | bytes 1179656 | tf_op jit(solution)/shard_map/ppermute | solution.py:76
  43.9 18.7 %collective-permute-start.8 = (bf16[12,32,512]{2,1,0:T(8,128)(2,1)}, bf16[12,32,512]{2,1,0:T(8,128)(2,1)}, u32[]{:S(2)}, u32[]{:S(2)}) collective-permute-start(bf16[12,32,512]{2,1,0:T(8,128)(2,1)} %collective-permute-done.7.refs_2_), channel_id=1, source_target_pairs={{0,1},{1,0},{2,3},{3,2},{4,5},{5,4},{6,7},{7,6},{8,9},{9,8},{10,11... | collective-permute-start | bytes 1179656 | tf_op jit(solution)/shard_map/ppermute | solution.py:76
  44.6 18.5 %collective-permute-start.1 = (bf16[12,32,512]{2,1,0:T(8,128)(2,1)S(1)}, bf16[12,32,512]{2,1,0:T(8,128)(2,1)S(1)}, u32[]{:S(2)}, u32[]{:S(2)}) collective-permute-start(bf16[12,32,512]{2,1,0:T(8,128)(2,1)S(1)} %collective-permute-done.refs_4_), channel_id=1, source_target_pairs={{0,4},{1,5},{2,6},{3,7},{4,12},{5,13},{6,14},{7,15},{8,0},{9,1},{1... | collective-permute-start | bytes 1179656 | tf_op jit(solution)/shard_map/ppermute | solution.py:76
  50.3 2.8 %copy-start.2 = (bf16[192,32,512]{2,1,0:T(8,128)(2,1)S(1)}, bf16[192,32,512]{2,1,0:T(8,128)(2,1)}, u32[]{:S(2)}) copy-start(bf16[192,32,512]{2,1,0:T(8,128)(2,1)} %copy-done.1) | copy-start | bytes 18874372
  53.1 1.0 copy-start.9
  54.1 1.0 copy-start.15
  55.1 1.6 %copy-start.13 = (bf16[12,32,512]{2,1,0:T(8,128)(2,1)S(1)}, bf16[12,32,512]{2,1,0:T(8,128)(2,1)}, u32[]{:S(2)}) copy-start(bf16[12,32,512]{2,1,0:T(8,128)(2,1)} %copy-done.12) | copy-start | bytes 1179652
  55.1 1.6 %copy-start.29 = (s32[4,16]{1,0:T(4,128)S(1)}, s32[4,16]{1,0:T(4,128)}, u32[]{:S(2)}) copy-start(s32[4,16]{1,0:T(4,128)} %constant.29.clone.refs_1_) | copy-start | bytes 772
  55.1 25.7 %slice-start = ((s8[6291456]{0:T(1024)(128)(4,1)}), s8[4194304]{0:T(1024)(128)(4,1)S(1)}, s32[]{:S(2)}) async-start(s8[6291456]{0:T(1024)(128)(4,1)} %bitcast.7), calls=%async_computation | async-start | bytes 8388608
  56.4 24.5 %slice-start.1 = ((s8[6291456]{0:T(1024)(128)(4,1)}), s8[2097152]{0:T(1024)(128)(4,1)S(1)}, s32[]{:S(2)}) async-start(s8[6291456]{0:T(1024)(128)(4,1)} %bitcast.7), calls=%async_computation.1 | async-start | bytes 4194304
  56.4 8.4 %collective-permute-start.5 = (bf16[12,32,512]{2,1,0:T(8,128)(2,1)S(1)}, bf16[12,32,512]{2,1,0:T(8,128)(2,1)S(1)}, u32[]{:S(2)}, u32[]{:S(2)}) collective-permute-start(bf16[12,32,512]{2,1,0:T(8,128)(2,1)S(1)} %collective-permute-done.refs_4_), channel_id=1, source_target_pairs={{0,1},{1,0},{2,3},{3,2},{4,5},{5,4},{6,7},{7,6},{8,9},{9,8},{10,11... | collective-permute-start | bytes 1179656 | tf_op jit(solution)/shard_map/ppermute | solution.py:76
  58.3 2.7 %copy-start.3 = (bf16[192,32,512]{2,1,0:T(8,128)(2,1)}, bf16[192,32,512]{2,1,0:T(8,128)(2,1)S(1)}, u32[]{:S(2)}) copy-start(bf16[192,32,512]{2,1,0:T(8,128)(2,1)S(1)} %shard_map.270.refs_6_) | copy-start | bytes 18874372
  61.0 22.8 %copy-start.36 = (f32[2,512]{1,0:T(2,128)S(1)}, f32[2,512]{1,0:T(2,128)}, u32[]{:S(2)}) copy-start(f32[2,512]{1,0:T(2,128)} %param.37) | copy-start | bytes 12292
  61.0 22.8 %copy-start.37 = (f32[2,512]{1,0:T(2,128)S(1)}, f32[2,512]{1,0:T(2,128)}, u32[]{:S(2)}) copy-start(f32[2,512]{1,0:T(2,128)} %param.36) | copy-start | bytes 12292
  61.0 12.0 %collective-permute-start.22 = (bf16[12,32,512]{2,1,0:T(8,128)(2,1)S(1)}, bf16[12,32,512]{2,1,0:T(8,128)(2,1)S(1)}, u32[]{:S(2)}, u32[]{:S(2)}) collective-permute-start(bf16[12,32,512]{2,1,0:T(8,128)(2,1)S(1)} %collective-permute-done.10.refs_5_), channel_id=1, source_target_pairs={{0,2},{1,3},{2,0},{3,1},{4,6},{5,7},{6,4},{7,5},{8,10},{9,11},{10,... | collective-permute-start | bytes 1179656 | tf_op jit(solution)/shard_map/ppermute | solution.py:76
  62.6 10.5 %collective-permute-start.6 = (bf16[12,32,512]{2,1,0:T(8,128)(2,1)}, bf16[12,32,512]{2,1,0:T(8,128)(2,1)S(1)}, u32[]{:S(2)}, u32[]{:S(2)}) collective-permute-start(bf16[12,32,512]{2,1,0:T(8,128)(2,1)} %collective-permute-done.4.refs_2_), channel_id=1, source_target_pairs={{0,1},{1,0},{2,3},{3,2},{4,5},{5,4},{6,7},{7,6},{8,9},{9,8},{10,11... | collective-permute-start | bytes 1179656 | tf_op jit(solution)/shard_map/ppermute | solution.py:76
  62.6 18.2 %collective-permute-start.19 = (bf16[12,32,512]{2,1,0:T(8,128)(2,1)}, bf16[12,32,512]{2,1,0:T(8,128)(2,1)S(1)}, u32[]{:S(2)}, u32[]{:S(2)}) collective-permute-start(bf16[12,32,512]{2,1,0:T(8,128)(2,1)} %collective-permute-done.11.refs_5_), channel_id=1, source_target_pairs={{0,2},{1,3},{2,0},{3,1},{4,6},{5,7},{6,4},{7,5},{8,10},{9,11},{10,... | collective-permute-start | bytes 1179656 | tf_op jit(solution)/shard_map/ppermute | solution.py:76
  63.2 19.1 %collective-permute-start.2 = (bf16[12,32,512]{2,1,0:T(8,128)(2,1)S(1)}, bf16[12,32,512]{2,1,0:T(8,128)(2,1)S(1)}, u32[]{:S(2)}, u32[]{:S(2)}) collective-permute-start(bf16[12,32,512]{2,1,0:T(8,128)(2,1)S(1)} %collective-permute-done.1.refs_5_), channel_id=1, source_target_pairs={{0,4},{1,5},{2,6},{3,7},{4,12},{5,13},{6,14},{7,15},{8,0},{9,1},{1... | collective-permute-start | bytes 1179656 | tf_op jit(solution)/shard_map/ppermute | solution.py:76
  64.7 20.4 %collective-permute-start.23 = (bf16[12,32,512]{2,1,0:T(8,128)(2,1)S(1)}, bf16[12,32,512]{2,1,0:T(8,128)(2,1)S(1)}, u32[]{:S(2)}, u32[]{:S(2)}) collective-permute-start(bf16[12,32,512]{2,1,0:T(8,128)(2,1)S(1)} %collective-permute-done.10.refs_5_), channel_id=1, source_target_pairs={{0,1},{1,0},{2,3},{3,2},{4,5},{5,4},{6,7},{7,6},{8,9},{9,8},{10,11... | collective-permute-start | bytes 1179656 | tf_op jit(solution)/shard_map/ppermute | solution.py:76
  73.0 12.1 %collective-permute-start.24 = (bf16[12,32,512]{2,1,0:T(8,128)(2,1)S(1)}, bf16[12,32,512]{2,1,0:T(8,128)(2,1)S(1)}, u32[]{:S(2)}, u32[]{:S(2)}) collective-permute-start(bf16[12,32,512]{2,1,0:T(8,128)(2,1)S(1)} %collective-permute-done.22.refs_2_), channel_id=1, source_target_pairs={{0,1},{1,0},{2,3},{3,2},{4,5},{5,4},{6,7},{7,6},{8,9},{9,8},{10,11... | collective-permute-start | bytes 1179656 | tf_op jit(solution)/shard_map/ppermute | solution.py:76
  73.0 13.6 %collective-permute-start.20 = (bf16[12,32,512]{2,1,0:T(8,128)(2,1)}, bf16[12,32,512]{2,1,0:T(8,128)(2,1)S(1)}, u32[]{:S(2)}, u32[]{:S(2)}) collective-permute-start(bf16[12,32,512]{2,1,0:T(8,128)(2,1)} %collective-permute-done.11.refs_5_), channel_id=1, source_target_pairs={{0,1},{1,0},{2,3},{3,2},{4,5},{5,4},{6,7},{7,6},{8,9},{9,8},{10,11... | collective-permute-start | bytes 1179656 | tf_op jit(solution)/shard_map/ppermute | solution.py:76
  80.8 5.9 %collective-permute-start.21 = (bf16[12,32,512]{2,1,0:T(8,128)(2,1)S(1)}, bf16[12,32,512]{2,1,0:T(8,128)(2,1)S(1)}, u32[]{:S(2)}, u32[]{:S(2)}) collective-permute-start(bf16[12,32,512]{2,1,0:T(8,128)(2,1)S(1)} %collective-permute-done.19.refs_2_), channel_id=1, source_target_pairs={{0,1},{1,0},{2,3},{3,2},{4,5},{5,4},{6,7},{7,6},{8,9},{9,8},{10,11... | collective-permute-start | bytes 1179656 | tf_op jit(solution)/shard_map/ppermute | solution.py:76
  80.8 4.3 %slice-start.2 = ((s8[6291456]{0:T(1024)(128)(4,1)}), s8[4194304]{0:T(1024)(128)(4,1)S(1)}, s32[]{:S(2)}) async-start(s8[6291456]{0:T(1024)(128)(4,1)} %bitcast.9), calls=%async_computation.2 | async-start | bytes 8388608
  82.2 11.9 %collective-permute-start.28 = (bf16[12,32,512]{2,1,0:T(8,128)(2,1)S(1)}, bf16[12,32,512]{2,1,0:T(8,128)(2,1)S(1)}, u32[]{:S(2)}, u32[]{:S(2)}) collective-permute-start(bf16[12,32,512]{2,1,0:T(8,128)(2,1)S(1)} %collective-permute-done.1.refs_5_), channel_id=1, source_target_pairs={{0,2},{1,3},{2,0},{3,1},{4,6},{5,7},{6,4},{7,5},{8,10},{9,11},{10,... | collective-permute-start | bytes 1179656 | tf_op jit(solution)/shard_map/ppermute | solution.py:76
  83.8 1.7 %slice-start.3 = ((s8[6291456]{0:T(1024)(128)(4,1)}), s8[2097152]{0:T(1024)(128)(4,1)S(1)}, s32[]{:S(2)}) async-start(s8[6291456]{0:T(1024)(128)(4,1)} %bitcast.9), calls=%async_computation.3 | async-start | bytes 4194304
  83.8 1.7 %copy-start.28 = (s32[4,16]{1,0:T(4,128)S(1)}, s32[4,16]{1,0:T(4,128)}, u32[]{:S(2)}) copy-start(s32[4,16]{1,0:T(4,128)} %constant.30.clone.refs_1_) | copy-start | bytes 772
  85.1 1.6 %copy-start.27 = (s32[3,16]{1,0:T(4,128)S(1)}, s32[3,16]{1,0:T(4,128)}, u32[]{:S(2)}) copy-start(s32[3,16]{1,0:T(4,128)} %constant.31.clone.refs_1_) | copy-start | bytes 580
  93.5 11.3 %collective-permute-start.25 = (bf16[12,32,512]{2,1,0:T(8,128)(2,1)S(1)}, bf16[12,32,512]{2,1,0:T(8,128)(2,1)S(1)}, u32[]{:S(2)}, u32[]{:S(2)}) collective-permute-start(bf16[12,32,512]{2,1,0:T(8,128)(2,1)S(1)} %collective-permute-done.2.refs_5_), channel_id=1, source_target_pairs={{0,2},{1,3},{2,0},{3,1},{4,6},{5,7},{6,4},{7,5},{8,10},{9,11},{10,... | collective-permute-start | bytes 1179656 | tf_op jit(solution)/shard_map/ppermute | solution.py:76
  94.1 11.3 %collective-permute-start.29 = (bf16[12,32,512]{2,1,0:T(8,128)(2,1)S(1)}, bf16[12,32,512]{2,1,0:T(8,128)(2,1)S(1)}, u32[]{:S(2)}, u32[]{:S(2)}) collective-permute-start(bf16[12,32,512]{2,1,0:T(8,128)(2,1)S(1)} %collective-permute-done.1.refs_5_), channel_id=1, source_target_pairs={{0,1},{1,0},{2,3},{3,2},{4,5},{5,4},{6,7},{7,6},{8,9},{9,8},{10,11... | collective-permute-start | bytes 1179656 | tf_op jit(solution)/shard_map/ppermute | solution.py:76
  94.1 14.7 %collective-permute-start.30 = (bf16[12,32,512]{2,1,0:T(8,128)(2,1)S(1)}, bf16[12,32,512]{2,1,0:T(8,128)(2,1)S(1)}, u32[]{:S(2)}, u32[]{:S(2)}) collective-permute-start(bf16[12,32,512]{2,1,0:T(8,128)(2,1)S(1)} %collective-permute-done.28.refs_2_), channel_id=1, source_target_pairs={{0,1},{1,0},{2,3},{3,2},{4,5},{5,4},{6,7},{7,6},{8,9},{9,8},{10,11... | collective-permute-start | bytes 1179656 | tf_op jit(solution)/shard_map/ppermute | solution.py:76
  94.7 16.1 %collective-permute-start.26 = (bf16[12,32,512]{2,1,0:T(8,128)(2,1)S(1)}, bf16[12,32,512]{2,1,0:T(8,128)(2,1)S(1)}, u32[]{:S(2)}, u32[]{:S(2)}) collective-permute-start(bf16[12,32,512]{2,1,0:T(8,128)(2,1)S(1)} %collective-permute-done.2.refs_5_), channel_id=1, source_target_pairs={{0,1},{1,0},{2,3},{3,2},{4,5},{5,4},{6,7},{7,6},{8,9},{9,8},{10,11... | collective-permute-start | bytes 1179656 | tf_op jit(solution)/shard_map/ppermute | solution.py:76
  104.8 6.0 %collective-permute-start.27 = (bf16[12,32,512]{2,1,0:T(8,128)(2,1)S(1)}, bf16[12,32,512]{2,1,0:T(8,128)(2,1)S(1)}, u32[]{:S(2)}, u32[]{:S(2)}) collective-permute-start(bf16[12,32,512]{2,1,0:T(8,128)(2,1)S(1)} %collective-permute-done.25.refs_2_), channel_id=1, source_target_pairs={{0,1},{1,0},{2,3},{3,2},{4,5},{5,4},{6,7},{7,6},{8,9},{9,8},{10,11... | collective-permute-start | bytes 1179656 | tf_op jit(solution)/shard_map/ppermute | solution.py:76
  104.8 6.7 %collective-permute-start.31 = (bf16[72,512]{1,0:T(8,128)(2,1)S(1)}, bf16[72,512]{1,0:T(8,128)(2,1)S(1)}, u32[]{:S(2)}, u32[]{:S(2)}) collective-permute-start(bf16[72,512]{1,0:T(8,128)(2,1)S(1)} %get-tuple-element.62), channel_id=1, source_target_pairs={{0,16},{16,0},{1,17},{17,1},{2,18},{18,2},{3,19},{19,3},{4,20},{20... | collective-permute-start | bytes 221192 | tf_op jit(solution)/shard_map/ppermute | solution.py:76
  105.4 6.0 %collective-permute-start.32 = (bf16[72,512]{1,0:T(8,128)(2,1)S(1)}, bf16[72,512]{1,0:T(8,128)(2,1)S(1)}, u32[]{:S(2)}, u32[]{:S(2)}) collective-permute-start(bf16[72,512]{1,0:T(8,128)(2,1)S(1)} %get-tuple-element.63), channel_id=1, source_target_pairs={{0,15},{1,0},{2,1},{3,2},{4,3},{5,4},{6,5},{7,6},{8,7},{9,8},{10,9... | collective-permute-start | bytes 221192 | tf_op jit(solution)/shard_map/ppermute | solution.py:273
  108.9 3.8 %collective-permute-start.33 = (bf16[72,512]{1,0:T(8,128)(2,1)S(1)}, bf16[72,512]{1,0:T(8,128)(2,1)S(1)}, u32[]{:S(2)}, u32[]{:S(2)}) collective-permute-start(bf16[72,512]{1,0:T(8,128)(2,1)S(1)} %get-tuple-element.64), channel_id=1, source_target_pairs={{0,31},{1,16},{2,17},{3,18},{4,19},{5,20},{6,21},{7,22},{8,23},{9,... | collective-permute-start | bytes 221192 | tf_op jit(solution)/shard_map/ppermute | solution.py:275
  111.4 15.7 %copy-start.23 = (s32[288,1]{1,0:T(8,128)S(1)}, s32[288,1]{1,0:T(8,128)}, u32[]{:S(2)}) copy-start(s32[288,1]{1,0:T(8,128)} %constant.32.clone.pick) | copy-start | bytes 3460
  118.9 7.4 %collective-permute-start.34 = (bf16[72,512]{1,0:T(8,128)(2,1)S(1)}, bf16[72,512]{1,0:T(8,128)(2,1)S(1)}, u32[]{:S(2)}, u32[]{:S(2)}) collective-permute-start(bf16[72,512]{1,0:T(8,128)(2,1)S(1)} %get-tuple-element.65), channel_id=1, source_target_pairs={{0,17},{1,18},{2,19},{3,20},{4,21},{5,22},{6,23},{7,24},{8,25},{9,... | collective-permute-start | bytes 221192 | tf_op jit(solution)/shard_map/ppermute | solution.py:275
  118.9 8.2 %collective-permute-start.35 = (bf16[72,512]{1,0:T(8,128)(2,1)S(1)}, bf16[72,512]{1,0:T(8,128)(2,1)S(1)}, u32[]{:S(2)}, u32[]{:S(2)}) collective-permute-start(bf16[72,512]{1,0:T(8,128)(2,1)S(1)} %get-tuple-element.66), channel_id=1, source_target_pairs={{0,1},{1,2},{2,3},{3,4},{4,5},{5,6},{6,7},{7,8},{8,9},{9,10},{10,1... | collective-permute-start | bytes 221192 | tf_op jit(solution)/shard_map/ppermute | solution.py:273
  119.0 8.1 %collective-permute-start.36 = (bf16[72,512]{1,0:T(8,128)(2,1)S(1)}, bf16[72,512]{1,0:T(8,128)(2,1)S(1)}, u32[]{:S(2)}, u32[]{:S(2)}) collective-permute-start(bf16[72,512]{1,0:T(8,128)(2,1)S(1)} %get-tuple-element.67), channel_id=1, source_target_pairs={{0,16},{16,0},{1,17},{17,1},{2,18},{18,2},{3,19},{19,3},{4,20},{20... | collective-permute-start | bytes 221192 | tf_op jit(solution)/shard_map/ppermute | solution.py:76
  (15 other events, 12.1 us)
where the time goes:
time: 129 us; the launch traced here: 128 us
  waiting for transfers between devices  43 us (33%)
  Pallas kernels  29.6 us (23%)
  starting transfers between devices  28.3 us (22%)
  local copies, waits for them, and re-layouts  26.7 us (21%)
    ppermute x33, waiting for transfers between devices, over(): lax.ppermute(array, axis, [(i, fn(i)) for i in range(lax.axis_size(axis))])  35.2 us
    pallas_call x18, Pallas kernels, call(): pl.pallas_call(body, out_shape=out_shape, in_specs=[sspec() if i in smem...  29.6 us
    unnamed x84, local copies, waits for them, and re-layouts  26.5 us
    ppermute x33, starting transfers between devices, over(): lax.ppermute(array, axis, [(i, fn(i)) for i in range(lax.axis_size(axis))])  23.5 us
    ppermute x2, waiting for transfers between devices, roll_quarters(): three = lax.ppermute(quarters[0 if sign < 0 else 3], ('lev', 'lat'), flat)  6.91 us
    ppermute x2, starting transfers between devices, roll_quarters(): one = lax.ppermute(quarters[1 if sign < 0 else 2], 'lat', pairs)  3.5 us
  transfers between devices with their start and end apart: 37, of which 9 were waited for; matrix products, arithmetic and copies ran while one was open for 0% of the time, Pallas kernels for 17%

commit v1 on v0

--- a/solution.py
+++ b/solution.py
@@ -97,7 +97,7 @@
     return call(body, whole, args + [w], smem=(0, 1), limit=2, alias={len(args): 0})
 
 
-def gather(where, own, tie):
+def gather(where, own, early=(), tie=()):
     size = lax.axis_size("lat")
     outer = size // 4
     order = [0] + list(range(1, outer, 2)) + list(range(2, outer, 2))[::-1]
@@ -117,14 +117,16 @@
         if step:
             fresh.append((over("lat", lambda i: i ^ 1, tied), at ^ 1))
         w = place(where, w, waiting + ([(tied, at)] if step else []))
+        if last:
+            across, tie = lax.optimization_barrier((across, tie))
         waiting = fresh + [(over("lat", lambda i: i ^ 1, across), at ^ 3)]
         if not last:
             array = ahead
             tied, w = lax.optimization_barrier((ahead, w))
             if step == outer - 2:
-                tied, tie = lax.optimization_barrier((tied, tie))
+                tied, early = lax.optimization_barrier((tied, early))
             at = before[at // 4] * 4 + at % 4
-    return place(where, w, waiting), tie
+    return place(where, w, waiting), early, tie
 
 
 def prep_body(lev, ids, source, tokens, table, own, send):
@@ -332,9 +334,9 @@
         limit=16,
     )
     labels = regions.reshape(2, rows // 2, 2, cols // 2, 2, 2).transpose(4, 0, 2, 5, 1, 3).reshape(2, -1)
-    first, (state, labels) = gather(where, packed[0], (state, labels))
+    first, (labels,), _ = gather(where, packed[0], early=(labels,))
     plain = swin_block(first, gain_one[:1], gain_two[:1], [state], ())
-    second, plain = gather(where, packed[1], tuple(plain))
+    second, _, plain = gather(where, packed[1], tie=tuple(plain))
     rolled = roll_quarters(plain, -1)
     shifted = swin_block(second, gain_one[1:], gain_two[1:], rolled, (labels,))
     quarters = roll_quarters(shifted, 1)

time: 129 us -> 126 us (0.977)
  local copies, waits for them, and re-layouts: 26.7 us -> 22.6 us
  waiting for transfers between devices: 43 us -> 45.8 us
  Pallas kernels: 29.6 us -> 27.4 us
    unnamed x84 -> x70, local copies, waits for them, and re-layouts: 26.5 us -> 19 us
    reshape x3, local copies, waits for them, and re-layouts: 0.2 us -> 3.62 us  [local(): regions.reshape(2, rows // 2, 2, cols // 2, 2, 2)]
    ppermute x33, waiting for transfers between devices: 35.2 us -> 38.4 us  [over(): lax.ppermute(array, axis, [(i, fn(i)) for i in range(lax.axis_size(axis))])]
    ppermute x2, starting transfers between devices: 3.5 us -> 0.7 us  [roll_quarters(): one = lax.ppermute(quarters[1 if sign < 0 else 2], 'lat', pairs)]
    ppermute x33, starting transfers between devices: 23.5 us -> 26.3 us  [over(): lax.ppermute(array, axis, [(i, fn(i)) for i in range(lax.axis_size(axis))])]
    pallas_call x18, Pallas kernels: 29.6 us -> 27.4 us  [call(): pl.pallas_call(body, out_shape=out_shape, in_specs=[sspec() if i in smem...]
  transfers between devices with their start and end apart: 37 -> 37, of which waited for: 9 -> 11; matrix products, arithmetic and copies ran while one was open for 0% -> 3% of each run, Pallas kernels for 17% -> 15%
where the time goes in v1:
time: 126 us; the launch traced here: 125 us
  waiting for transfers between devices  45.8 us (36%)
  starting transfers between devices  28.7 us (23%)
  Pallas kernels  27.4 us (22%)
  local copies, waits for them, and re-layouts  22.6 us (18%)
    ppermute x33, waiting for transfers between devices, over(): lax.ppermute(array, axis, [(i, fn(i)) for i in range(lax.axis_size(axis))])  38.4 us
    pallas_call x18, Pallas kernels, call(): pl.pallas_call(body, out_shape=out_shape, in_specs=[sspec() if i in smem...  27.4 us
    ppermute x33, starting transfers between devices, over(): lax.ppermute(array, axis, [(i, fn(i)) for i in range(lax.axis_size(axis))])  26.3 us
    unnamed x70, local copies, waits for them, and re-layouts  19 us
    ppermute x2, waiting for transfers between devices, roll_quarters(): three = lax.ppermute(quarters[0 if sign < 0 else 3], ('lev', 'lat'), flat)  7.39 us
    reshape x3, local copies, waits for them, and re-layouts, local(): regions.reshape(2, rows // 2, 2, cols // 2, 2, 2)  3.62 us
  transfers between devices with their start and end apart: 37, of which 11 were waited for; matrix products, arithmetic and copies ran while one was open for 3% of the time, Pallas kernels for 15%

profile of v1, /device:TPU:0, one launch (start us, length us, event | category | flops | bytes accessed | tf_op | source)
XLA Modules:
  0.0 125.0 jit_solution(6062920104887635765)
XLA Ops:
  0.0 1.0 copy-done.14
  1.0 0.9 copy-done.15
  1.9 0.9 copy-done.16
  2.8 0.8 copy-done.18
  3.7 0.8 shard_map.262
  5.0 2.6 %collective-permute-start.11 = (bf16[12,32,512]{2,1,0:T(8,128)(2,1)}, bf16[12,32,512]{2,1,0:T(8,128)(2,1)S(1)}, u32[]{:S(2)}, u32[]{:S(2)}) collective-permute-start(bf16[12,32,512]{2,1,0:T(8,128)(2,1)} %get-tuple-element.42.refs_2_), channel_id=1, source_target_pairs={{0,4},{1,5},{2,6},{3,7},{4,12},{5,13},{6,14},{7,15},{8,0},{9,1},{1... | collective-permute-start | bytes 1179656 | tf_op jit(solution)/shard_map/ppermute | solution.py:76
  7.8 2.6 %collective-permute-start = (bf16[12,32,512]{2,1,0:T(8,128)(2,1)S(1)}, bf16[12,32,512]{2,1,0:T(8,128)(2,1)S(1)}, u32[]{:S(2)}, u32[]{:S(2)}) collective-permute-start(bf16[12,32,512]{2,1,0:T(8,128)(2,1)S(1)} %get-tuple-element.36.refs_2_), channel_id=1, source_target_pairs={{0,4},{1,5},{2,6},{3,7},{4,12},{5,13},{6,14},{7,15},{8,0},{9,1},{1... | collective-permute-start | bytes 1179656 | tf_op jit(solution)/shard_map/ppermute | solution.py:76
  10.4 1.5 %collective-permute-start.7 = (bf16[12,32,512]{2,1,0:T(8,128)(2,1)S(1)}, bf16[12,32,512]{2,1,0:T(8,128)(2,1)S(1)}, u32[]{:S(2)}, u32[]{:S(2)}) collective-permute-start(bf16[12,32,512]{2,1,0:T(8,128)(2,1)S(1)} %get-tuple-element.36.refs_2_), channel_id=1, source_target_pairs={{0,2},{1,3},{2,0},{3,1},{4,6},{5,7},{6,4},{7,5},{8,10},{9,11},{10,... | collective-permute-start | bytes 1179656 | tf_op jit(solution)/shard_map/ppermute | solution.py:76
  11.9 0.5 collective-permute-start.18
  12.5 0.7 copy-done.27
  13.1 1.0 shard_map.267.refs_3_
  14.2 0.6 shard_map.268.refs_5_
  14.8 2.7 %copy-done.1 = bf16[192,32,512]{2,1,0:T(8,128)(2,1)} copy-done((bf16[192,32,512]{2,1,0:T(8,128)(2,1)}, bf16[192,32,512]{2,1,0:T(8,128)(2,1)S(1)}, u32[]{:S(2)}) %copy-start.1) | copy-done | bytes 6291480
  17.5 1.2 collective-permute-done.11.refs_4_
  18.7 1.9 %collective-permute-start.15 = (bf16[12,32,512]{2,1,0:T(8,128)(2,1)S(1)}, bf16[12,32,512]{2,1,0:T(8,128)(2,1)S(1)}, u32[]{:S(2)}, u32[]{:S(2)}) collective-permute-start(bf16[12,32,512]{2,1,0:T(8,128)(2,1)S(1)} %collective-permute-done.11.refs_4_), channel_id=1, source_target_pairs={{0,2},{1,3},{2,0},{3,1},{4,6},{5,7},{6,4},{7,5},{8,10},{9,11},{10,... | collective-permute-start | bytes 1179656 | tf_op jit(solution)/shard_map/ppermute | solution.py:76
  20.6 0.9 collective-permute-start.12
  21.5 0.6 shard_map.263.refs_3_
  22.1 0.6 shard_map.264.refs_5_
  22.7 2.6 %copy-done = bf16[192,32,512]{2,1,0:T(8,128)(2,1)} copy-done((bf16[192,32,512]{2,1,0:T(8,128)(2,1)}, bf16[192,32,512]{2,1,0:T(8,128)(2,1)S(1)}, u32[]{:S(2)}) %copy-start) | copy-done | bytes 6291480
  25.3 1.9 %collective-permute-done.refs_4_ = bf16[12,32,512]{2,1,0:T(8,128)(2,1)S(1)} collective-permute-done((bf16[12,32,512]{2,1,0:T(8,128)(2,1)S(1)}, bf16[12,32,512]{2,1,0:T(8,128)(2,1)S(1)}, u32[]{:S(2)}, u32[]{:S(2)}) %collective-permute-start) | collective-permute-done | bytes 393248 | tf_op jit(solution)/shard_map/ppermute | solution.py:76
  27.2 1.9 %collective-permute-start.4 = (bf16[12,32,512]{2,1,0:T(8,128)(2,1)S(1)}, bf16[12,32,512]{2,1,0:T(8,128)(2,1)S(1)}, u32[]{:S(2)}, u32[]{:S(2)}) collective-permute-start(bf16[12,32,512]{2,1,0:T(8,128)(2,1)S(1)} %collective-permute-done.refs_4_), channel_id=1, source_target_pairs={{0,2},{1,3},{2,0},{3,1},{4,6},{5,7},{6,4},{7,5},{8,10},{9,11},{10,... | collective-permute-start | bytes 1179656 | tf_op jit(solution)/shard_map/ppermute | solution.py:76
  29.0 1.8 %collective-permute-done.18.refs_2_ = bf16[12,32,512]{2,1,0:T(8,128)(2,1)S(1)} collective-permute-done((bf16[12,32,512]{2,1,0:T(8,128)(2,1)}, bf16[12,32,512]{2,1,0:T(8,128)(2,1)S(1)}, u32[]{:S(2)}, u32[]{:S(2)}) %collective-permute-start.18) | collective-permute-done | bytes 393248 | tf_op jit(solution)/shard_map/ppermute | solution.py:76
  30.8 0.5 collective-permute-start.16
  31.3 7.9 %collective-permute-done.15.refs_2_ = bf16[12,32,512]{2,1,0:T(8,128)(2,1)S(1)} collective-permute-done((bf16[12,32,512]{2,1,0:T(8,128)(2,1)S(1)}, bf16[12,32,512]{2,1,0:T(8,128)(2,1)S(1)}, u32[]{:S(2)}, u32[]{:S(2)}) %collective-permute-start.15) | collective-permute-done | bytes 393248 | tf_op jit(solution)/shard_map/ppermute | solution.py:76
  39.7 7.0 %collective-permute-done.4.refs_2_ = bf16[12,32,512]{2,1,0:T(8,128)(2,1)S(1)} collective-permute-done((bf16[12,32,512]{2,1,0:T(8,128)(2,1)S(1)}, bf16[12,32,512]{2,1,0:T(8,128)(2,1)S(1)}, u32[]{:S(2)}, u32[]{:S(2)}) %collective-permute-start.4) | collective-permute-done | bytes 393248 | tf_op jit(solution)/shard_map/ppermute | solution.py:76
  46.7 0.7 copy-done.8
  47.9 0.8 copy-done.10
  48.9 0.7 copy-done.12
  49.9 1.4 %reshape.7 = s32[2,3,2,6,2,2]{3,2,5,4,1,0:T(2,128)} reshape(s32[6,12,4]{1,2,0:T(4,128)} %param.35) | data formatting | bytes 2304 | tf_op jit(solution)/shard_map/reshape | solution.py:336
  51.3 1.4 %copy.42 = s32[2,3,2,6,2,2]{3,1,5,2,0,4:T(4,128)} copy(s32[2,3,2,6,2,2]{3,2,5,4,1,0:T(2,128)} %reshape.7) | data formatting | bytes 2304 | tf_op jit(solution)/shard_map/reshape | solution.py:336
  52.7 0.9 reshape.8.refs_3_
  53.5 2.8 %copy-done.2 = bf16[192,32,512]{2,1,0:T(8,128)(2,1)S(1)} copy-done((bf16[192,32,512]{2,1,0:T(8,128)(2,1)S(1)}, bf16[192,32,512]{2,1,0:T(8,128)(2,1)}, u32[]{:S(2)}) %copy-start.2) | copy-done | bytes 6291480
  56.3 1.0 copy-done.9
  57.3 0.7 shard_map.269.refs_6_
  58.4 0.7 shard_map.270.refs_6_
  59.1 2.7 %copy-done.3 = bf16[192,32,512]{2,1,0:T(8,128)(2,1)} copy-done((bf16[192,32,512]{2,1,0:T(8,128)(2,1)}, bf16[192,32,512]{2,1,0:T(8,128)(2,1)S(1)}, u32[]{:S(2)}) %copy-start.3) | copy-done | bytes 6291480
  61.9 1.6 %collective-permute-start.23 = (bf16[12,32,512]{2,1,0:T(8,128)(2,1)S(1)}, bf16[12,32,512]{2,1,0:T(8,128)(2,1)S(1)}, u32[]{:S(2)}, u32[]{:S(2)}) collective-permute-start(bf16[12,32,512]{2,1,0:T(8,128)(2,1)S(1)} %collective-permute-done.12.refs_5_), channel_id=1, source_target_pairs={{0,2},{1,3},{2,0},{3,1},{4,6},{5,7},{6,4},{7,5},{8,10},{9,11},{10,... | collective-permute-start | bytes 1179656 | tf_op jit(solution)/shard_map/ppermute | solution.py:76
  63.4 0.5 collective-permute-start.20
  64.2 1.1 shard_map.265.refs_6_
  65.4 1.6 %collective-permute-start.28 = (bf16[12,32,512]{2,1,0:T(8,128)(2,1)S(1)}, bf16[12,32,512]{2,1,0:T(8,128)(2,1)S(1)}, u32[]{:S(2)}, u32[]{:S(2)}) collective-permute-start(bf16[12,32,512]{2,1,0:T(8,128)(2,1)S(1)} %collective-permute-done.1.refs_5_), channel_id=1, source_target_pairs={{0,2},{1,3},{2,0},{3,1},{4,6},{5,7},{6,4},{7,5},{8,10},{9,11},{10,... | collective-permute-start | bytes 1179656 | tf_op jit(solution)/shard_map/ppermute | solution.py:76
  67.0 0.9 shard_map.273
  68.1 1.6 %collective-permute-start.26 = (bf16[4,72,512]{2,1,0:T(8,128)(2,1)S(1)}, bf16[4,72,512]{2,1,0:T(8,128)(2,1)S(1)}, u32[]{:S(2)}, u32[]{:S(2)}) collective-permute-start(bf16[4,72,512]{2,1,0:T(8,128)(2,1)S(1)} %get-tuple-element.51), channel_id=1, source_target_pairs={{0,16},{16,0},{1,17},{17,1},{2,18},{18,2},{3,19},{19,3},{4,20},{20... | collective-permute-start | bytes 884744 | tf_op jit(solution)/shard_map/ppermute | solution.py:76
  69.6 4.3 %collective-permute-done.23.refs_2_ = bf16[12,32,512]{2,1,0:T(8,128)(2,1)S(1)} collective-permute-done((bf16[12,32,512]{2,1,0:T(8,128)(2,1)S(1)}, bf16[12,32,512]{2,1,0:T(8,128)(2,1)S(1)}, u32[]{:S(2)}, u32[]{:S(2)}) %collective-permute-start.23) | collective-permute-done | bytes 393248 | tf_op jit(solution)/shard_map/ppermute | solution.py:76
  73.9 8.4 %collective-permute-done.20.refs_2_ = bf16[12,32,512]{2,1,0:T(8,128)(2,1)S(1)} collective-permute-done((bf16[12,32,512]{2,1,0:T(8,128)(2,1)S(1)}, bf16[12,32,512]{2,1,0:T(8,128)(2,1)S(1)}, u32[]{:S(2)}, u32[]{:S(2)}) %collective-permute-start.20) | collective-permute-done | bytes 393248 | tf_op jit(solution)/shard_map/ppermute | solution.py:76
  82.3 1.2 shard_map.266.refs_6_
  83.6 0.6 collective-permute-start.21
  84.3 5.8 %collective-permute-done.28.refs_2_ = bf16[12,32,512]{2,1,0:T(8,128)(2,1)S(1)} collective-permute-done((bf16[12,32,512]{2,1,0:T(8,128)(2,1)S(1)}, bf16[12,32,512]{2,1,0:T(8,128)(2,1)S(1)}, u32[]{:S(2)}, u32[]{:S(2)}) %collective-permute-start.28) | collective-permute-done | bytes 393248 | tf_op jit(solution)/shard_map/ppermute | solution.py:76
  90.0 1.5 %collective-permute-start.9 = (bf16[12,32,512]{2,1,0:T(8,128)(2,1)S(1)}, bf16[12,32,512]{2,1,0:T(8,128)(2,1)S(1)}, u32[]{:S(2)}, u32[]{:S(2)}) collective-permute-start(bf16[12,32,512]{2,1,0:T(8,128)(2,1)S(1)} %collective-permute-done.2.refs_5_), channel_id=1, source_target_pairs={{0,2},{1,3},{2,0},{3,1},{4,6},{5,7},{6,4},{7,5},{8,10},{9,11},{10,... | collective-permute-start | bytes 1179656 | tf_op jit(solution)/shard_map/ppermute | solution.py:76
  91.6 0.5 collective-permute-start.30
  92.1 3.2 %shard_map.274.refs_3_ = bf16[288,512]{1,0:T(8,128)(2,1)S(1)} custom-call(bf16[4,72,512]{2,1,0:T(8,128)(2,1)S(1)} %get-tuple-element.50.own, bf16[4,72,512]{2,1,0:T(8,128)(2,1)S(1)} %collective-permute-done.26.recv, bf16[4,512]{1,0:T(4,128)(2,1)S(1)} %copy-done.25, bf16[512,512]{1,0:T(8,128)(2,1)S(1)} %copy-done.6, bf16[512,1024]{1,0:T(8,128)(2,1)S(1)} %copy-done.4, ...), custom_call_target="tpu_custom_call" | custom-call | tf_op jit(solution)/shard_map/pallas_call | solution.py:35
  95.3 0.7 shard_map.271.refs_5_
  96.2 0.7 shard_map.272.refs_0_
  96.8 6.1 %shard_map.275 = (bf16[72,512]{1,0:T(8,128)(2,1)S(1)}, bf16[72,512]{1,0:T(8,128)(2,1)S(1)}, bf16[72,512]{1,0:T(8,128)(2,1)S(1)}, bf16[72,512]{1,0:T(8,128)(2,1)S(1)}) custom-call(bf16[192,32,512]{2,1,0:T(8,128)(2,1)S(1)} %shard_map.272.refs_0_, f32[1,512]{1,0:T(1,128)S(1)} %get-tuple-element.71.refs_1_, f32[1,512]{1,0:T(1,128)S(1)} %get-tuple-element.68.refs_2_, ...), custom_call_target="tpu_custom_call" | custom-call | tf_op jit(solution)/shard_map/pallas_call | solution.py:35
  103.5 1.5 %collective-permute-start.31 = (bf16[72,512]{1,0:T(8,128)(2,1)S(1)}, bf16[72,512]{1,0:T(8,128)(2,1)S(1)}, u32[]{:S(2)}, u32[]{:S(2)}) collective-permute-start(bf16[72,512]{1,0:T(8,128)(2,1)S(1)} %get-tuple-element.60), channel_id=1, source_target_pairs={{0,16},{16,0},{1,17},{17,1},{2,18},{18,2},{3,19},{19,3},{4,20},{20... | collective-permute-start | bytes 221192 | tf_op jit(solution)/shard_map/ppermute | solution.py:76
  105.0 0.7 collective-permute-start.32
  105.7 0.7 collective-permute-start.33
  106.4 0.7 shard_map.276.refs_5_
  107.1 0.7 shard_map.277.refs_0_
  107.8 1.6 %collective-permute-done.33.refs_7_ = bf16[72,512]{1,0:T(8,128)(2,1)S(1)} collective-permute-done((bf16[72,512]{1,0:T(8,128)(2,1)S(1)}, bf16[72,512]{1,0:T(8,128)(2,1)S(1)}, u32[]{:S(2)}, u32[]{:S(2)}) %collective-permute-start.33) | collective-permute-done | bytes 73760 | tf_op jit(solution)/shard_map/ppermute | solution.py:277
  109.5 6.2 %shard_map.278 = (bf16[72,512]{1,0:T(8,128)(2,1)S(1)}, bf16[72,512]{1,0:T(8,128)(2,1)S(1)}, bf16[72,512]{1,0:T(8,128)(2,1)S(1)}, bf16[72,512]{1,0:T(8,128)(2,1)S(1)}) custom-call(bf16[192,32,512]{2,1,0:T(8,128)(2,1)S(1)} %shard_map.277.refs_0_, f32[1,512]{1,0:T(1,128)S(1)} %get-tuple-element.72.refs_1_, f32[1,512]{1,0:T(1,128)S(1)} %get-tuple-element.67.refs_2_, ...), custom_call_target="tpu_custom_call" | custom-call | tf_op jit(solution)/shard_map/pallas_call | solution.py:35
  115.7 1.0 collective-permute-start.34
  116.7 1.5 %collective-permute-start.36 = (bf16[72,512]{1,0:T(8,128)(2,1)S(1)}, bf16[72,512]{1,0:T(8,128)(2,1)S(1)}, u32[]{:S(2)}, u32[]{:S(2)}) collective-permute-start(bf16[72,512]{1,0:T(8,128)(2,1)S(1)} %get-tuple-element.65), channel_id=1, source_target_pairs={{0,16},{16,0},{1,17},{17,1},{2,18},{18,2},{3,19},{19,3},{4,20},{20... | collective-permute-start | bytes 221192 | tf_op jit(solution)/shard_map/ppermute | solution.py:76
  118.2 5.8 %collective-permute-done.34.refs_0_ = bf16[72,512]{1,0:T(8,128)(2,1)S(1)} collective-permute-done((bf16[72,512]{1,0:T(8,128)(2,1)S(1)}, bf16[72,512]{1,0:T(8,128)(2,1)S(1)}, u32[]{:S(2)}, u32[]{:S(2)}) %collective-permute-start.34) | collective-permute-done | bytes 73760 | tf_op jit(solution)/shard_map/ppermute | solution.py:277
  123.9 1.1 shard_map.279
  (105 shorter events, 4.0 us)
Async XLA Ops:
  0.0 14.2 %copy-start.26 = (s32[1,16]{1,0:T(1,128)S(1)}, s32[1,16]{1,0:T(1,128)}, u32[]{:S(2)}) copy-start(s32[1,16]{1,0:T(1,128)} %constant.27.clone.refs_1_) | copy-start | bytes 196
  0.0 1.0 copy-start.14
  4.5 7.4 %collective-permute-start.14 = (bf16[12,32,512]{2,1,0:T(8,128)(2,1)}, bf16[12,32,512]{2,1,0:T(8,128)(2,1)S(1)}, u32[]{:S(2)}, u32[]{:S(2)}) collective-permute-start(bf16[12,32,512]{2,1,0:T(8,128)(2,1)} %get-tuple-element.42.refs_2_), channel_id=1, source_target_pairs={{0,1},{1,0},{2,3},{3,2},{4,5},{5,4},{6,7},{7,6},{8,9},{9,8},{10,11... | collective-permute-start | bytes 1179656 | tf_op jit(solution)/shard_map/ppermute | solution.py:76
  5.0 13.8 %collective-permute-start.11 = (bf16[12,32,512]{2,1,0:T(8,128)(2,1)}, bf16[12,32,512]{2,1,0:T(8,128)(2,1)S(1)}, u32[]{:S(2)}, u32[]{:S(2)}) collective-permute-start(bf16[12,32,512]{2,1,0:T(8,128)(2,1)} %get-tuple-element.42.refs_2_), channel_id=1, source_target_pairs={{0,4},{1,5},{2,6},{3,7},{4,12},{5,13},{6,14},{7,15},{8,0},{9,1},{1... | collective-permute-start | bytes 1179656 | tf_op jit(solution)/shard_map/ppermute | solution.py:76
  7.6 13.0 %collective-permute-start.3 = (bf16[12,32,512]{2,1,0:T(8,128)(2,1)S(1)}, bf16[12,32,512]{2,1,0:T(8,128)(2,1)S(1)}, u32[]{:S(2)}, u32[]{:S(2)}) collective-permute-start(bf16[12,32,512]{2,1,0:T(8,128)(2,1)S(1)} %get-tuple-element.36.refs_2_), channel_id=1, source_target_pairs={{0,1},{1,0},{2,3},{3,2},{4,5},{5,4},{6,7},{7,6},{8,9},{9,8},{10,11... | collective-permute-start | bytes 1179656 | tf_op jit(solution)/shard_map/ppermute | solution.py:76
  7.8 19.4 %collective-permute-start = (bf16[12,32,512]{2,1,0:T(8,128)(2,1)S(1)}, bf16[12,32,512]{2,1,0:T(8,128)(2,1)S(1)}, u32[]{:S(2)}, u32[]{:S(2)}) collective-permute-start(bf16[12,32,512]{2,1,0:T(8,128)(2,1)S(1)} %get-tuple-element.36.refs_2_), channel_id=1, source_target_pairs={{0,4},{1,5},{2,6},{3,7},{4,12},{5,13},{6,14},{7,15},{8,0},{9,1},{1... | collective-permute-start | bytes 1179656 | tf_op jit(solution)/shard_map/ppermute | solution.py:76
  10.4 20.4 %collective-permute-start.7 = (bf16[12,32,512]{2,1,0:T(8,128)(2,1)S(1)}, bf16[12,32,512]{2,1,0:T(8,128)(2,1)S(1)}, u32[]{:S(2)}, u32[]{:S(2)}) collective-permute-start(bf16[12,32,512]{2,1,0:T(8,128)(2,1)S(1)} %get-tuple-element.36.refs_2_), channel_id=1, source_target_pairs={{0,2},{1,3},{2,0},{3,1},{4,6},{5,7},{6,4},{7,5},{8,10},{9,11},{10,... | collective-permute-start | bytes 1179656 | tf_op jit(solution)/shard_map/ppermute | solution.py:76
  11.9 18.9 %collective-permute-start.18 = (bf16[12,32,512]{2,1,0:T(8,128)(2,1)}, bf16[12,32,512]{2,1,0:T(8,128)(2,1)S(1)}, u32[]{:S(2)}, u32[]{:S(2)}) collective-permute-start(bf16[12,32,512]{2,1,0:T(8,128)(2,1)} %get-tuple-element.42.refs_2_), channel_id=1, source_target_pairs={{0,2},{1,3},{2,0},{3,1},{4,6},{5,7},{6,4},{7,5},{8,10},{9,11},{10,... | collective-permute-start | bytes 1179656 | tf_op jit(solution)/shard_map/ppermute | solution.py:76
  14.8 2.7 %copy-start.1 = (bf16[192,32,512]{2,1,0:T(8,128)(2,1)}, bf16[192,32,512]{2,1,0:T(8,128)(2,1)S(1)}, u32[]{:S(2)}) copy-start(bf16[192,32,512]{2,1,0:T(8,128)(2,1)S(1)} %shard_map.268.refs_5_) | copy-start | bytes 18874372
  18.7 20.5 %collective-permute-start.15 = (bf16[12,32,512]{2,1,0:T(8,128)(2,1)S(1)}, bf16[12,32,512]{2,1,0:T(8,128)(2,1)S(1)}, u32[]{:S(2)}, u32[]{:S(2)}) collective-permute-start(bf16[12,32,512]{2,1,0:T(8,128)(2,1)S(1)} %collective-permute-done.11.refs_4_), channel_id=1, source_target_pairs={{0,2},{1,3},{2,0},{3,1},{4,6},{5,7},{6,4},{7,5},{8,10},{9,11},{10,... | collective-permute-start | bytes 1179656 | tf_op jit(solution)/shard_map/ppermute | solution.py:76
  20.6 18.6 %collective-permute-start.12 = (bf16[12,32,512]{2,1,0:T(8,128)(2,1)S(1)}, bf16[12,32,512]{2,1,0:T(8,128)(2,1)S(1)}, u32[]{:S(2)}, u32[]{:S(2)}) collective-permute-start(bf16[12,32,512]{2,1,0:T(8,128)(2,1)S(1)} %collective-permute-done.11.refs_4_), channel_id=1, source_target_pairs={{0,4},{1,5},{2,6},{3,7},{4,12},{5,13},{6,14},{7,15},{8,0},{9,1},{1... | collective-permute-start | bytes 1179656 | tf_op jit(solution)/shard_map/ppermute | solution.py:76
  22.1 31.5 %copy-start.24 = (s32[3,16]{1,0:T(4,128)S(1)}, s32[3,16]{1,0:T(4,128)}, u32[]{:S(2)}) copy-start(s32[3,16]{1,0:T(4,128)} %constant.28.clone.refs_1_) | copy-start | bytes 580
  22.7 2.6 %copy-start = (bf16[192,32,512]{2,1,0:T(8,128)(2,1)}, bf16[192,32,512]{2,1,0:T(8,128)(2,1)S(1)}, u32[]{:S(2)}) copy-start(bf16[192,32,512]{2,1,0:T(8,128)(2,1)S(1)} %shard_map.264.refs_5_) | copy-start | bytes 18874372
  27.2 19.5 %collective-permute-start.4 = (bf16[12,32,512]{2,1,0:T(8,128)(2,1)S(1)}, bf16[12,32,512]{2,1,0:T(8,128)(2,1)S(1)}, u32[]{:S(2)}, u32[]{:S(2)}) collective-permute-start(bf16[12,32,512]{2,1,0:T(8,128)(2,1)S(1)} %collective-permute-done.refs_4_), channel_id=1, source_target_pairs={{0,2},{1,3},{2,0},{3,1},{4,6},{5,7},{6,4},{7,5},{8,10},{9,11},{10,... | collective-permute-start | bytes 1179656 | tf_op jit(solution)/shard_map/ppermute | solution.py:76
  30.8 15.9 %collective-permute-start.19 = (bf16[12,32,512]{2,1,0:T(8,128)(2,1)S(1)}, bf16[12,32,512]{2,1,0:T(8,128)(2,1)S(1)}, u32[]{:S(2)}, u32[]{:S(2)}) collective-permute-start(bf16[12,32,512]{2,1,0:T(8,128)(2,1)S(1)} %collective-permute-done.18.refs_2_), channel_id=1, source_target_pairs={{0,1},{1,0},{2,3},{3,2},{4,5},{5,4},{6,7},{7,6},{8,9},{9,8},{10,11... | collective-permute-start | bytes 1179656 | tf_op jit(solution)/shard_map/ppermute | solution.py:76
  30.8 17.1 %collective-permute-start.16 = (bf16[12,32,512]{2,1,0:T(8,128)(2,1)S(1)}, bf16[12,32,512]{2,1,0:T(8,128)(2,1)S(1)}, u32[]{:S(2)}, u32[]{:S(2)}) collective-permute-start(bf16[12,32,512]{2,1,0:T(8,128)(2,1)S(1)} %collective-permute-done.11.refs_4_), channel_id=1, source_target_pairs={{0,1},{1,0},{2,3},{3,2},{4,5},{5,4},{6,7},{7,6},{8,9},{9,8},{10,11... | collective-permute-start | bytes 1179656 | tf_op jit(solution)/shard_map/ppermute | solution.py:76
  39.2 9.7 %collective-permute-start.17 = (bf16[12,32,512]{2,1,0:T(8,128)(2,1)S(1)}, bf16[12,32,512]{2,1,0:T(8,128)(2,1)S(1)}, u32[]{:S(2)}, u32[]{:S(2)}) collective-permute-start(bf16[12,32,512]{2,1,0:T(8,128)(2,1)S(1)} %collective-permute-done.15.refs_2_), channel_id=1, source_target_pairs={{0,1},{1,0},{2,3},{3,2},{4,5},{5,4},{6,7},{7,6},{8,9},{9,8},{10,11... | collective-permute-start | bytes 1179656 | tf_op jit(solution)/shard_map/ppermute | solution.py:76
  39.2 22.6 %collective-permute-start.13 = (bf16[12,32,512]{2,1,0:T(8,128)(2,1)S(1)}, bf16[12,32,512]{2,1,0:T(8,128)(2,1)S(1)}, u32[]{:S(2)}, u32[]{:S(2)}) collective-permute-start(bf16[12,32,512]{2,1,0:T(8,128)(2,1)S(1)} %collective-permute-done.12.refs_5_), channel_id=1, source_target_pairs={{0,4},{1,5},{2,6},{3,7},{4,12},{5,13},{6,14},{7,15},{8,0},{9,1},{1... | collective-permute-start | bytes 1179656 | tf_op jit(solution)/shard_map/ppermute | solution.py:76
  46.7 16.8 %collective-permute-start.8 = (bf16[12,32,512]{2,1,0:T(8,128)(2,1)S(1)}, bf16[12,32,512]{2,1,0:T(8,128)(2,1)}, u32[]{:S(2)}, u32[]{:S(2)}) collective-permute-start(bf16[12,32,512]{2,1,0:T(8,128)(2,1)S(1)} %collective-permute-done.7.refs_2_), channel_id=1, source_target_pairs={{0,1},{1,0},{2,3},{3,2},{4,5},{5,4},{6,7},{7,6},{8,9},{9,8},{10,11... | collective-permute-start | bytes 1179656 | tf_op jit(solution)/shard_map/ppermute | solution.py:76
  47.4 16.5 %collective-permute-start.1 = (bf16[12,32,512]{2,1,0:T(8,128)(2,1)S(1)}, bf16[12,32,512]{2,1,0:T(8,128)(2,1)S(1)}, u32[]{:S(2)}, u32[]{:S(2)}) collective-permute-start(bf16[12,32,512]{2,1,0:T(8,128)(2,1)S(1)} %collective-permute-done.refs_4_), channel_id=1, source_target_pairs={{0,4},{1,5},{2,6},{3,7},{4,12},{5,13},{6,14},{7,15},{8,0},{9,1},{1... | collective-permute-start | bytes 1179656 | tf_op jit(solution)/shard_map/ppermute | solution.py:76
  48.6 16.7 %collective-permute-start.5 = (bf16[12,32,512]{2,1,0:T(8,128)(2,1)S(1)}, bf16[12,32,512]{2,1,0:T(8,128)(2,1)}, u32[]{:S(2)}, u32[]{:S(2)}) collective-permute-start(bf16[12,32,512]{2,1,0:T(8,128)(2,1)S(1)} %collective-permute-done.refs_4_), channel_id=1, source_target_pairs={{0,1},{1,0},{2,3},{3,2},{4,5},{5,4},{6,7},{7,6},{8,9},{9,8},{10,11... | collective-permute-start | bytes 1179656 | tf_op jit(solution)/shard_map/ppermute | solution.py:76
  49.6 18.3 %collective-permute-start.6 = (bf16[12,32,512]{2,1,0:T(8,128)(2,1)S(1)}, bf16[12,32,512]{2,1,0:T(8,128)(2,1)}, u32[]{:S(2)}, u32[]{:S(2)}) collective-permute-start(bf16[12,32,512]{2,1,0:T(8,128)(2,1)S(1)} %collective-permute-done.4.refs_2_), channel_id=1, source_target_pairs={{0,1},{1,0},{2,3},{3,2},{4,5},{5,4},{6,7},{7,6},{8,9},{9,8},{10,11... | collective-permute-start | bytes 1179656 | tf_op jit(solution)/shard_map/ppermute | solution.py:76
  53.5 2.8 %copy-start.2 = (bf16[192,32,512]{2,1,0:T(8,128)(2,1)S(1)}, bf16[192,32,512]{2,1,0:T(8,128)(2,1)}, u32[]{:S(2)}) copy-start(bf16[192,32,512]{2,1,0:T(8,128)(2,1)} %copy-done.1) | copy-start | bytes 18874372
  56.3 1.0 copy-start.9
  57.3 1.0 copy-start.11
  57.3 1.1 copy-start.13
  57.3 1.1 copy-start.23
  57.3 6.9 %slice-start = ((s8[6291456]{0:T(1024)(128)(4,1)}), s8[4194304]{0:T(1024)(128)(4,1)S(1)}, s32[]{:S(2)}) async-start(s8[6291456]{0:T(1024)(128)(4,1)} %bitcast.7), calls=%async_computation | async-start | bytes 8388608
  58.4 5.8 %slice-start.1 = ((s8[6291456]{0:T(1024)(128)(4,1)}), s8[2097152]{0:T(1024)(128)(4,1)S(1)}, s32[]{:S(2)}) async-start(s8[6291456]{0:T(1024)(128)(4,1)} %bitcast.7), calls=%async_computation.1 | async-start | bytes 4194304
  59.1 2.7 %copy-start.3 = (bf16[192,32,512]{2,1,0:T(8,128)(2,1)}, bf16[192,32,512]{2,1,0:T(8,128)(2,1)S(1)}, u32[]{:S(2)}) copy-start(bf16[192,32,512]{2,1,0:T(8,128)(2,1)S(1)} %shard_map.270.refs_6_) | copy-start | bytes 18874372
  61.8 5.2 %copy-start.5 = (bf16[4,6,24,512]{3,2,1,0:T(8,128)(2,1)S(1)}, bf16[4,6,24,512]{3,2,1,0:T(8,128)(2,1)}, u32[]{:S(2)}) copy-start(bf16[4,6,24,512]{3,2,1,0:T(8,128)(2,1)} %tokens.1) | copy-start | bytes 1769476
  61.8 5.2 %copy-start.19 = (s32[72,1]{1,0:T(8,128)S(1)}, s32[72,1]{1,0:T(8,128)}, u32[]{:S(2)}) copy-start(s32[72,1]{1,0:T(8,128)} %constant.25.clone.source) | copy-start | bytes 868
  61.8 5.2 %copy-start.20 = (f32[13,512]{1,0:T(8,128)S(1)}, f32[13,512]{1,0:T(8,128)}, u32[]{:S(2)}) copy-start(f32[13,512]{1,0:T(8,128)} %table.1) | copy-start | bytes 79876
  61.8 5.2 %copy-start.28 = (s32[4]{0:T(128)S(1)}, s32[4]{0:T(128)}, u32[]{:S(2)}) copy-start(s32[4]{0:T(128)} %ids.1) | copy-start | bytes 52
  61.9 12.1 %collective-permute-start.23 = (bf16[12,32,512]{2,1,0:T(8,128)(2,1)S(1)}, bf16[12,32,512]{2,1,0:T(8,128)(2,1)S(1)}, u32[]{:S(2)}, u32[]{:S(2)}) collective-permute-start(bf16[12,32,512]{2,1,0:T(8,128)(2,1)S(1)} %collective-permute-done.12.refs_5_), channel_id=1, source_target_pairs={{0,2},{1,3},{2,0},{3,1},{4,6},{5,7},{6,4},{7,5},{8,10},{9,11},{10,... | collective-permute-start | bytes 1179656 | tf_op jit(solution)/shard_map/ppermute | solution.py:76
  63.4 18.9 %collective-permute-start.20 = (bf16[12,32,512]{2,1,0:T(8,128)(2,1)S(1)}, bf16[12,32,512]{2,1,0:T(8,128)(2,1)S(1)}, u32[]{:S(2)}, u32[]{:S(2)}) collective-permute-start(bf16[12,32,512]{2,1,0:T(8,128)(2,1)S(1)} %collective-permute-done.13.refs_5_), channel_id=1, source_target_pairs={{0,2},{1,3},{2,0},{3,1},{4,6},{5,7},{6,4},{7,5},{8,10},{9,11},{10,... | collective-permute-start | bytes 1179656 | tf_op jit(solution)/shard_map/ppermute | solution.py:76
  64.0 20.2 %collective-permute-start.2 = (bf16[12,32,512]{2,1,0:T(8,128)(2,1)S(1)}, bf16[12,32,512]{2,1,0:T(8,128)(2,1)S(1)}, u32[]{:S(2)}, u32[]{:S(2)}) collective-permute-start(bf16[12,32,512]{2,1,0:T(8,128)(2,1)S(1)} %collective-permute-done.1.refs_5_), channel_id=1, source_target_pairs={{0,4},{1,5},{2,6},{3,7},{4,12},{5,13},{6,14},{7,15},{8,0},{9,1},{1... | collective-permute-start | bytes 1179656 | tf_op jit(solution)/shard_map/ppermute | solution.py:76
  65.4 24.7 %collective-permute-start.28 = (bf16[12,32,512]{2,1,0:T(8,128)(2,1)S(1)}, bf16[12,32,512]{2,1,0:T(8,128)(2,1)S(1)}, u32[]{:S(2)}, u32[]{:S(2)}) collective-permute-start(bf16[12,32,512]{2,1,0:T(8,128)(2,1)S(1)} %collective-permute-done.1.refs_5_), channel_id=1, source_target_pairs={{0,2},{1,3},{2,0},{3,1},{4,6},{5,7},{6,4},{7,5},{8,10},{9,11},{10,... | collective-permute-start | bytes 1179656 | tf_op jit(solution)/shard_map/ppermute | solution.py:76
  68.0 27.3 %slice-start.2 = ((s8[6291456]{0:T(1024)(128)(4,1)}), s8[4194304]{0:T(1024)(128)(4,1)S(1)}, s32[]{:S(2)}) async-start(s8[6291456]{0:T(1024)(128)(4,1)} %bitcast.9), calls=%async_computation.2 | async-start | bytes 8388608
  68.0 24.1 %copy-start.29 = (f32[2,512]{1,0:T(2,128)S(1)}, f32[2,512]{1,0:T(2,128)}, u32[]{:S(2)}) copy-start(f32[2,512]{1,0:T(2,128)} %param.37) | copy-start | bytes 12292
  68.0 24.1 %copy-start.30 = (f32[2,512]{1,0:T(2,128)S(1)}, f32[2,512]{1,0:T(2,128)}, u32[]{:S(2)}) copy-start(f32[2,512]{1,0:T(2,128)} %param.36) | copy-start | bytes 12292
  68.0 24.1 %copy-start.4 = (bf16[512,1024]{1,0:T(8,128)(2,1)S(1)}, bf16[512,1024]{1,0:T(8,128)(2,1)}, u32[]{:S(2)}) copy-start(bf16[512,1024]{1,0:T(8,128)(2,1)} %w_kv.1) | copy-start | bytes 3145732
  68.0 24.1 %copy-start.6 = (bf16[512,512]{1,0:T(8,128)(2,1)S(1)}, bf16[512,512]{1,0:T(8,128)(2,1)}, u32[]{:S(2)}) copy-start(bf16[512,512]{1,0:T(8,128)(2,1)} %w_query.1) | copy-start | bytes 1572868
  68.0 24.1 %copy-start.7 = (bf16[512,512]{1,0:T(8,128)(2,1)S(1)}, bf16[512,512]{1,0:T(8,128)(2,1)}, u32[]{:S(2)}) copy-start(bf16[512,512]{1,0:T(8,128)(2,1)} %w_out.1) | copy-start | bytes 1572868
  68.0 24.1 %copy-start.25 = (bf16[4,512]{1,0:T(4,128)(2,1)S(1)}, bf16[4,512]{1,0:T(4,128)(2,1)}, u32[]{:S(2)}) copy-start(bf16[4,512]{1,0:T(4,128)(2,1)} %latent_query.1) | copy-start | bytes 12292
  68.0 27.3 %slice-start.3 = ((s8[6291456]{0:T(1024)(128)(4,1)}), s8[2097152]{0:T(1024)(128)(4,1)S(1)}, s32[]{:S(2)}) async-start(s8[6291456]{0:T(1024)(128)(4,1)} %bitcast.9), calls=%async_computation.3 | async-start | bytes 4194304
  68.1 27.3 %copy-start.22 = (s32[4,16]{1,0:T(4,128)S(1)}, s32[4,16]{1,0:T(4,128)}, u32[]{:S(2)}) copy-start(s32[4,16]{1,0:T(4,128)} %constant.30.clone.refs_1_) | copy-start | bytes 772
  68.1 15.5 %collective-permute-start.26 = (bf16[4,72,512]{2,1,0:T(8,128)(2,1)S(1)}, bf16[4,72,512]{2,1,0:T(8,128)(2,1)S(1)}, u32[]{:S(2)}, u32[]{:S(2)}) collective-permute-start(bf16[4,72,512]{2,1,0:T(8,128)(2,1)S(1)} %get-tuple-element.51), channel_id=1, source_target_pairs={{0,16},{16,0},{1,17},{17,1},{2,18},{18,2},{3,19},{19,3},{4,20},{20... | collective-permute-start | bytes 884744 | tf_op jit(solution)/shard_map/ppermute | solution.py:76
  73.9 17.6 %collective-permute-start.24 = (bf16[12,32,512]{2,1,0:T(8,128)(2,1)S(1)}, bf16[12,32,512]{2,1,0:T(8,128)(2,1)S(1)}, u32[]{:S(2)}, u32[]{:S(2)}) collective-permute-start(bf16[12,32,512]{2,1,0:T(8,128)(2,1)S(1)} %collective-permute-done.12.refs_5_), channel_id=1, source_target_pairs={{0,1},{1,0},{2,3},{3,2},{4,5},{5,4},{6,7},{7,6},{8,9},{9,8},{10,11... | collective-permute-start | bytes 1179656 | tf_op jit(solution)/shard_map/ppermute | solution.py:76
  82.3 9.2 %collective-permute-start.25 = (bf16[12,32,512]{2,1,0:T(8,128)(2,1)S(1)}, bf16[12,32,512]{2,1,0:T(8,128)(2,1)S(1)}, u32[]{:S(2)}, u32[]{:S(2)}) collective-permute-start(bf16[12,32,512]{2,1,0:T(8,128)(2,1)S(1)} %collective-permute-done.23.refs_2_), channel_id=1, source_target_pairs={{0,1},{1,0},{2,3},{3,2},{4,5},{5,4},{6,7},{7,6},{8,9},{9,8},{10,11... | collective-permute-start | bytes 1179656 | tf_op jit(solution)/shard_map/ppermute | solution.py:76
  83.6 12.4 %collective-permute-start.21 = (bf16[12,32,512]{2,1,0:T(8,128)(2,1)S(1)}, bf16[12,32,512]{2,1,0:T(8,128)(2,1)S(1)}, u32[]{:S(2)}, u32[]{:S(2)}) collective-permute-start(bf16[12,32,512]{2,1,0:T(8,128)(2,1)S(1)} %collective-permute-done.13.refs_5_), channel_id=1, source_target_pairs={{0,1},{1,0},{2,3},{3,2},{4,5},{5,4},{6,7},{7,6},{8,9},{9,8},{10,11... | collective-permute-start | bytes 1179656 | tf_op jit(solution)/shard_map/ppermute | solution.py:76
  84.2 12.0 %collective-permute-start.22 = (bf16[12,32,512]{2,1,0:T(8,128)(2,1)S(1)}, bf16[12,32,512]{2,1,0:T(8,128)(2,1)S(1)}, u32[]{:S(2)}, u32[]{:S(2)}) collective-permute-start(bf16[12,32,512]{2,1,0:T(8,128)(2,1)S(1)} %collective-permute-done.20.refs_2_), channel_id=1, source_target_pairs={{0,1},{1,0},{2,3},{3,2},{4,5},{5,4},{6,7},{7,6},{8,9},{9,8},{10,11... | collective-permute-start | bytes 1179656 | tf_op jit(solution)/shard_map/ppermute | solution.py:76
  90.0 12.9 %collective-permute-start.9 = (bf16[12,32,512]{2,1,0:T(8,128)(2,1)S(1)}, bf16[12,32,512]{2,1,0:T(8,128)(2,1)S(1)}, u32[]{:S(2)}, u32[]{:S(2)}) collective-permute-start(bf16[12,32,512]{2,1,0:T(8,128)(2,1)S(1)} %collective-permute-done.2.refs_5_), channel_id=1, source_target_pairs={{0,2},{1,3},{2,0},{3,1},{4,6},{5,7},{6,4},{7,5},{8,10},{9,11},{10,... | collective-permute-start | bytes 1179656 | tf_op jit(solution)/shard_map/ppermute | solution.py:76
  91.5 13.4 %collective-permute-start.29 = (bf16[12,32,512]{2,1,0:T(8,128)(2,1)S(1)}, bf16[12,32,512]{2,1,0:T(8,128)(2,1)S(1)}, u32[]{:S(2)}, u32[]{:S(2)}) collective-permute-start(bf16[12,32,512]{2,1,0:T(8,128)(2,1)S(1)} %collective-permute-done.1.refs_5_), channel_id=1, source_target_pairs={{0,1},{1,0},{2,3},{3,2},{4,5},{5,4},{6,7},{7,6},{8,9},{9,8},{10,11... | collective-permute-start | bytes 1179656 | tf_op jit(solution)/shard_map/ppermute | solution.py:76
  91.6 14.1 %collective-permute-start.30 = (bf16[12,32,512]{2,1,0:T(8,128)(2,1)S(1)}, bf16[12,32,512]{2,1,0:T(8,128)(2,1)S(1)}, u32[]{:S(2)}, u32[]{:S(2)}) collective-permute-start(bf16[12,32,512]{2,1,0:T(8,128)(2,1)S(1)} %collective-permute-done.28.refs_2_), channel_id=1, source_target_pairs={{0,1},{1,0},{2,3},{3,2},{4,5},{5,4},{6,7},{7,6},{8,9},{9,8},{10,11... | collective-permute-start | bytes 1179656 | tf_op jit(solution)/shard_map/ppermute | solution.py:76
  96.0 11.0 %collective-permute-start.10 = (bf16[12,32,512]{2,1,0:T(8,128)(2,1)S(1)}, bf16[12,32,512]{2,1,0:T(8,128)(2,1)S(1)}, u32[]{:S(2)}, u32[]{:S(2)}) collective-permute-start(bf16[12,32,512]{2,1,0:T(8,128)(2,1)S(1)} %collective-permute-done.2.refs_5_), channel_id=1, source_target_pairs={{0,1},{1,0},{2,3},{3,2},{4,5},{5,4},{6,7},{7,6},{8,9},{9,8},{10,11... | collective-permute-start | bytes 1179656 | tf_op jit(solution)/shard_map/ppermute | solution.py:76
  103.0 4.1 %collective-permute-start.27 = (bf16[12,32,512]{2,1,0:T(8,128)(2,1)S(1)}, bf16[12,32,512]{2,1,0:T(8,128)(2,1)S(1)}, u32[]{:S(2)}, u32[]{:S(2)}) collective-permute-start(bf16[12,32,512]{2,1,0:T(8,128)(2,1)S(1)} %collective-permute-done.9.refs_2_), channel_id=1, source_target_pairs={{0,1},{1,0},{2,3},{3,2},{4,5},{5,4},{6,7},{7,6},{8,9},{9,8},{10,11... | collective-permute-start | bytes 1179656 | tf_op jit(solution)/shard_map/ppermute | solution.py:76
  103.5 4.4 %collective-permute-start.31 = (bf16[72,512]{1,0:T(8,128)(2,1)S(1)}, bf16[72,512]{1,0:T(8,128)(2,1)S(1)}, u32[]{:S(2)}, u32[]{:S(2)}) collective-permute-start(bf16[72,512]{1,0:T(8,128)(2,1)S(1)} %get-tuple-element.60), channel_id=1, source_target_pairs={{0,16},{16,0},{1,17},{17,1},{2,18},{18,2},{3,19},{19,3},{4,20},{20... | collective-permute-start | bytes 221192 | tf_op jit(solution)/shard_map/ppermute | solution.py:76
  105.0 2.9 %collective-permute-start.32 = (bf16[72,512]{1,0:T(8,128)(2,1)S(1)}, bf16[72,512]{1,0:T(8,128)(2,1)S(1)}, u32[]{:S(2)}, u32[]{:S(2)}) collective-permute-start(bf16[72,512]{1,0:T(8,128)(2,1)S(1)} %get-tuple-element.61), channel_id=1, source_target_pairs={{0,15},{1,0},{2,1},{3,2},{4,3},{5,4},{6,5},{7,6},{8,7},{9,8},{10,9... | collective-permute-start | bytes 221192 | tf_op jit(solution)/shard_map/ppermute | solution.py:275
  105.7 3.8 %collective-permute-start.33 = (bf16[72,512]{1,0:T(8,128)(2,1)S(1)}, bf16[72,512]{1,0:T(8,128)(2,1)S(1)}, u32[]{:S(2)}, u32[]{:S(2)}) collective-permute-start(bf16[72,512]{1,0:T(8,128)(2,1)S(1)} %get-tuple-element.62), channel_id=1, source_target_pairs={{0,31},{1,16},{2,17},{3,18},{4,19},{5,20},{6,21},{7,22},{8,23},{9,... | collective-permute-start | bytes 221192 | tf_op jit(solution)/shard_map/ppermute | solution.py:277
  107.7 16.2 %copy-start.17 = (s32[288,1]{1,0:T(8,128)S(1)}, s32[288,1]{1,0:T(8,128)}, u32[]{:S(2)}) copy-start(s32[288,1]{1,0:T(8,128)} %constant.32.clone.pick) | copy-start | bytes 3460
  115.7 8.2 %collective-permute-start.34 = (bf16[72,512]{1,0:T(8,128)(2,1)S(1)}, bf16[72,512]{1,0:T(8,128)(2,1)S(1)}, u32[]{:S(2)}, u32[]{:S(2)}) collective-permute-start(bf16[72,512]{1,0:T(8,128)(2,1)S(1)} %get-tuple-element.63), channel_id=1, source_target_pairs={{0,17},{1,18},{2,19},{3,20},{4,21},{5,22},{6,23},{7,24},{8,25},{9,... | collective-permute-start | bytes 221192 | tf_op jit(solution)/shard_map/ppermute | solution.py:277
  116.7 7.3 %collective-permute-start.35 = (bf16[72,512]{1,0:T(8,128)(2,1)S(1)}, bf16[72,512]{1,0:T(8,128)(2,1)S(1)}, u32[]{:S(2)}, u32[]{:S(2)}) collective-permute-start(bf16[72,512]{1,0:T(8,128)(2,1)S(1)} %get-tuple-element.64), channel_id=1, source_target_pairs={{0,1},{1,2},{2,3},{3,4},{4,5},{5,6},{6,7},{7,8},{8,9},{9,10},{10,1... | collective-permute-start | bytes 221192 | tf_op jit(solution)/shard_map/ppermute | solution.py:275
  116.7 7.3 %collective-permute-start.36 = (bf16[72,512]{1,0:T(8,128)(2,1)S(1)}, bf16[72,512]{1,0:T(8,128)(2,1)S(1)}, u32[]{:S(2)}, u32[]{:S(2)}) collective-permute-start(bf16[72,512]{1,0:T(8,128)(2,1)S(1)} %get-tuple-element.65), channel_id=1, source_target_pairs={{0,16},{16,0},{1,17},{17,1},{2,18},{18,2},{3,19},{19,3},{4,20},{20... | collective-permute-start | bytes 221192 | tf_op jit(solution)/shard_map/ppermute | solution.py:76
  (8 other events, 6.5 us)
